TPU v7x, 256 devices: a whole 4x4x8 slice. The times are simulated.
256 devices in a mesh: rows: 256 (over z, y, x, core).
Axes of the slice: x: 4, y: 4, z: 8, core: 2. Of those that a mesh axis runs over, the one named last changes fastest.
Arguments:
- factor_b: float32 [131072, 512], P('rows'), may hold values from -6 to 6
- band_vals: float32 [64, 131072], P(None, 'rows'), may hold values from -0.3125 to 0.3125
- offsets: int32 [64], replicated, may hold values from -64 to 64, as said below
- sketch: float32 [1024, 512], replicated, may hold values from -0.1875 to 0.1875
Outputs:
- factor_z: float32 [131072, 512], P('rows')
Inputs may be any that keep to these rules, and one draw needn't show every extreme that they name: 64 distinct offsets; -64 and 64 are always among them.
All inputs are finite; a program needn't handle non-finite values.
Results may differ from a plain program's by a relative error of at most 0.0035.
Values sent between devices are 32-bit elements; how exact they have to be, the bound alone decides.
No kernel may reach another device: no remote copies, remote signals or barrier semaphores. Data moves between devices by JAX's collectives and lax.ppermute only.
A program may use at most 64 MiB of HBM per device.

v0:
```python
import jax
import jax.numpy as jnp
from jax import lax
from jax.experimental import pallas as pl
from jax.experimental.pallas import tpu as pltpu
from jax.sharding import Mesh
from jax.sharding import PartitionSpec as P

HALF = 64
ROWS = ("z", "y", "x", "c")
F32 = jnp.float32
BF16 = jnp.bfloat16
BLOCK = 128
PANEL = 16
VMEM = pl.BlockSpec(memory_space=pltpu.VMEM)
SMEM = pl.BlockSpec(memory_space=pltpu.SMEM)


def split2(x):
    h = x.astype(BF16)
    return h, (x - h.astype(F32)).astype(BF16)


def split3(x):
    h = x.astype(BF16)
    r = x - h.astype(F32)
    m = r.astype(BF16)
    return h, m, (r - m.astype(F32)).astype(BF16)


def mul(a, b, dims=(1, 0)):
    return lax.dot_general(a, b, (((dims[0],), (dims[1],)), ((), ())), preferred_element_type=F32)


def near_dot(a, b, dims=(1, 0)):
    return mul(a[0], b[0], dims) + (mul(a[0], b[1], dims) + mul(a[1], b[0], dims))


def exact_dot(a, b):
    ah, am, al = split3(a)
    bh, bm, bl = split3(b)
    hm = jnp.concatenate([ah, am], 1)
    low = mul(hm, jnp.concatenate([bm, bm], 0))
    low += mul(jnp.concatenate([al, ah], 1), jnp.concatenate([bh, bl], 0))
    return mul(hm, jnp.concatenate([bh, bh], 0)) + low


def factor_block(d_block):
    n = d_block.shape[0]
    count = n // PANEL
    row_ids = lax.broadcasted_iota(jnp.int32, (n, n), 0)
    eye = (row_ids == lax.broadcasted_iota(jnp.int32, (n, n), 1)).astype(F32)
    both = jnp.concatenate([d_block, eye], 1)
    panels = [both[PANEL * q : PANEL * (q + 1)] for q in range(count)]
    sub = lax.broadcasted_iota(jnp.int32, (PANEL, n), 0)
    inverse = []
    for p in range(count):
        a, b = panels[p][:, :n], panels[p][:, n:]
        at = PANEL * p
        cols = [jnp.broadcast_to(a[:, at + j : at + j + 1], (PANEL, n)) for j in range(PANEL)]
        w = jnp.zeros((PANEL, n), F32)
        for k in range(PANEL):
            m = cols[k]
            root = lax.rsqrt(m[k : k + 1])
            inv = root * root
            keep = sub == k
            w = jnp.where(keep, b[k : k + 1] * root, w)
            a = jnp.where(keep, a[k : k + 1] * inv, a - m * (a[k : k + 1] * inv))
            b = jnp.where(keep, b[k : k + 1] * inv, b - m * (b[k : k + 1] * inv))
            for j in range(k + 1, PANEL):
                c = cols[j][k : k + 1] * inv
                cols[j] = jnp.where(keep, c, cols[j] - m * c)
        inverse.append(w)
        if p + 1 < count:
            parts = [jnp.zeros((at, 2 * n), F32)] if p else []
            parts += [jnp.concatenate([a, b], 1), jnp.zeros((n - at - PANEL, 2 * n), F32)]
            left = jnp.concatenate([panels[q][:, :n] for q in range(p + 1, count)], 0)
            change = exact_dot(left, jnp.concatenate(parts, 0))
            for q in range(p + 1, count):
                i = PANEL * (q - p - 1)
                panels[q] = panels[q] - change[i : i + PANEL]
    return jnp.concatenate(inverse, 0)


def invert_factor(work_ref, row_ref, inv_ref):
    n = BLOCK
    count = work_ref.shape[0] // n
    lane = lax.broadcasted_iota(jnp.int32, (n, count * n), 1) // n

    def step(b, carry):
        at = pl.multiple_of(b * n, n)
        w = factor_block(work_ref[pl.ds(at, n), pl.ds(at, n)])
        row = exact_dot(w, work_ref[pl.ds(at, n), :])
        row = jnp.where(lane == b, jnp.concatenate([w] * count, 1), row)
        row_ref[...] = row
        high, low = split2(jnp.where(lane <= b, row, 0.0))
        inv_ref[0, pl.ds(at, n), :] = high
        inv_ref[1, pl.ds(at, n), :] = low

        def trail(i, carry):
            to = pl.multiple_of(i * n, n)
            left = row_ref[:, pl.ds(to, n)].T
            kept = jnp.where(lane == b, 0.0, work_ref[pl.ds(to, n), :])
            work_ref[pl.ds(to, n), :] = kept - exact_dot(left, row_ref[...])
            return carry

        lax.fori_loop(b + 1, count, trail, 0)
        return carry

    lax.fori_loop(0, count, step, 0)


def normal_matrix(own, rest, work_ref):
    size = work_ref.shape[0]
    parts = [split3(own), split3(rest)]
    for at in range(0, size, BLOCK):
        total = jnp.zeros((BLOCK, size - at), F32)
        for i, j in ((1, 1), (2, 0), (0, 2), (1, 0), (0, 1), (0, 0)):
            for side in parts:
                total += mul(side[i][:, at : at + BLOCK], side[j][:, at:], (0, 0))
        if at:
            work_ref[at : at + BLOCK, :at] = jnp.zeros((BLOCK, at), F32)
        work_ref[at : at + BLOCK, at:] = total


def powers_body(core, off, up, mid, down, v_up, v_mid, v_down, sketch, mine, other, parts, dense, long_ref):
    n = BLOCK
    size = mid.shape[0]
    width = mid.shape[1]
    lanes = lax.broadcasted_iota(jnp.int32, (off.shape[0], 2 * n), 1)
    hot = (off[...] + HALF == lanes).astype(BF16)
    hot = jnp.concatenate([hot, hot], 0)
    blocks = size // n + 2
    for i in range(blocks):
        if i == 0:
            v = v_up[...]
        elif i == blocks - 1:
            v = v_down[...]
        else:
            v = v_mid[:, n * (i - 1) : n * i]
        spread = mul(jnp.concatenate(split2(v), 0), hot, (0, 0))
        spread = pltpu.roll(spread, 0, 1, stride=1, stride_axis=0)
        dense[0, i], dense[1, i] = split2(spread)
    reach = 3 * HALF
    for half, (a, b, c) in enumerate(zip(split2(up[...]), split2(mid[...]), split2(down[...]))):
        long_ref[half, 0, :reach] = a
        long_ref[half, 0, reach : reach + size] = b
        long_ref[half, 0, reach + size :] = c
        parts[half, 0] = b
        edge = jnp.zeros((HALF, width), BF16)
        for level in (1, 2):
            long_ref[half, level, :HALF] = edge
            long_ref[half, level, size + 2 * reach - HALF :] = edge
    for level in range(3):
        for i in range(blocks) if level < 2 else range(1, blocks - 1):
            window = [long_ref[half, level, n * i : n * i + 2 * n] for half in range(2)]
            result = split2(near_dot((dense[0, i], dense[1, i]), window))
            for half in range(2):
                if level < 2:
                    long_ref[half, level + 1, n * i + HALF : n * i + HALF + n] = result[half]
                if 0 < i < blocks - 1:
                    parts[half, level + 1, n * (i - 1) : n * i] = result[half]
    gram_halves(core, parts, sketch, mine, other)


def gram_halves(core, parts, sketch, mine, other):
    size = parts.shape[2]
    top, low = (split2(sketch[size * s : size * (s + 1)]) for s in range(2))
    get = lambda s: (parts[0, s], parts[1, s])
    projected = split2(near_dot(get(0), top) + near_dot(get(1), low))
    c = core[0]
    mine[...] = near_dot(get(c), projected, (0, 0))
    other[...] = near_dot(get(1 - c), projected, (0, 0))


def next_body(core, own, rest, sketch, parts, mine, other, new_parts, work, row, inv):
    c = core[0]
    normal_matrix(own[...], rest[...], work)
    invert_factor(work, row, inv)
    sides = (split2(own[...]), split2(rest[...]))
    for s in range(2):
        reached = near_dot((parts[0, 2 * s + c], parts[1, 2 * s + c]), sides[0])
        reached += near_dot((parts[0, 2 * s + 1 - c], parts[1, 2 * s + 1 - c]), sides[1])
        result = near_dot(split2(reached), (inv[0], inv[1]), (1, 1))
        new_parts[0, s], new_parts[1, s] = split2(result)
    gram_halves(core, new_parts, sketch, mine, other)


def last_body(core, own, rest, parts, out, work, row, inv):
    c = core[0]
    normal_matrix(own[...], rest[...], work)
    invert_factor(work, row, inv)
    reached = near_dot((parts[0, c], parts[1, c]), split2(own[...]))
    reached += near_dot((parts[0, 1 - c], parts[1, 1 - c]), split2(rest[...]))
    out[...] = near_dot(split2(reached), (inv[0], inv[1]), (1, 1))


def shaped(*shape, dtype=F32):
    return jax.ShapeDtypeStruct(shape, dtype)


def inverse_scratch(width):
    return [
        pltpu.VMEM((width, width), F32),
        pltpu.VMEM((BLOCK, width), F32),
        pltpu.VMEM((2, width, width), BF16),
    ]


def powers(core, off, up, mid, down, v_up, v_mid, v_down, sketch):
    size, width = mid.shape
    return pl.pallas_call(
        powers_body,
        out_shape=(shaped(width, width), shaped(width, width), shaped(2, 4, size, width, dtype=BF16)),
        in_specs=[SMEM] + [VMEM] * 8,
        out_specs=(VMEM,) * 3,
        scratch_shapes=[
            pltpu.VMEM((2, size // BLOCK + 2, BLOCK, 2 * BLOCK), BF16),
            pltpu.VMEM((2, 3, size + 6 * HALF, width), BF16),
        ],
        name="powers",
    )(core, off, up, mid, down, v_up, v_mid, v_down, sketch)


def next_level(core, own, rest, sketch, parts):
    size, width = parts.shape[2:]
    return pl.pallas_call(
        next_body,
        out_shape=(shaped(width, width), shaped(width, width), shaped(2, 2, size, width, dtype=BF16)),
        in_specs=[SMEM] + [VMEM] * 4,
        out_specs=(VMEM,) * 3,
        scratch_shapes=inverse_scratch(width),
        name="next_level",
    )(core, own, rest, sketch, parts)


def last_level(core, own, rest, parts):
    size, width = parts.shape[2:]
    return pl.pallas_call(
        last_body,
        out_shape=shaped(size, width),
        in_specs=[SMEM] + [VMEM] * 3,
        out_specs=VMEM,
        scratch_shapes=inverse_scratch(width),
        name="last_level",
    )(core, own, rest, parts)


def swap_cores(x):
    return lax.ppermute(x, "c", [(0, 1), (1, 0)])


def sum_over_rows(mine, other):
    half = mine + swap_cores(other)
    plane = lax.axis_size("y") * lax.axis_size("x")
    rows, width = half.shape
    blocks = half.reshape(plane, rows // plane, width)
    part = lax.all_to_all(blocks, ("y", "x"), 0, 0, tiled=True).sum(0)
    size = lax.axis_size("z")
    for pairs in (
        [(i, i ^ 1) for i in range(size)],
        [(i, i ^ 2) for i in range(size)],
        [(i, size - 1 - i) for i in range(size)],
    ):
        part = part + lax.ppermute(part, "z", pairs)
    copies = jnp.broadcast_to(part[None], blocks.shape)
    own = lax.all_to_all(copies, ("y", "x"), 0, 0, tiled=True).reshape(rows, width)
    return own, swap_cores(own)


def from_neighbours(shard, dim, width):
    size, length = (lax.axis_size(ROWS), shard.shape[dim])
    up = [(i, i + 1) for i in range(size - 1)]
    down = [(j, i) for i, j in up]
    last = lax.slice_in_dim(shard, length - width, length, axis=dim)
    first = lax.slice_in_dim(shard, 0, width, axis=dim)
    return lax.ppermute(last, ROWS, up), lax.ppermute(first, ROWS, down)


def per_device(factor_b, band_vals, offsets, sketch):
    core = lax.axis_index("c").reshape(1)
    up, down = from_neighbours(factor_b, 0, 3 * HALF)
    v_up, v_down = from_neighbours(band_vals, 1, 2 * HALF)
    mine, other, parts = powers(
        core, offsets.reshape(-1, 1), up, factor_b, down, v_up, band_vals, v_down, sketch
    )
    own, rest = sum_over_rows(mine, other)
    mine, other, parts = next_level(core, own, rest, sketch, parts)
    own, rest = sum_over_rows(mine, other)
    return last_level(core, own, rest, parts)


def solution(mesh):
    split = Mesh(mesh.devices.reshape(8, 4, 4, 2), ROWS)
    return jax.shard_map(
        per_device,
        mesh=split,
        in_specs=(P(ROWS, None), P(None, ROWS), P(), P()),
        out_specs=P(ROWS, None),
        check_vma=False,
    )
```

profile of v0, /device:TPU:33, one launch (start us, length us, event | category | flops | bytes accessed | tf_op | source)
XLA Modules:
  0.0 224.5 jit_solution(985657372612111256)
XLA Ops:
  0.0 1.2 fusion
  1.2 2.6 %collective-permute-start.1 = (f32[192,512]{1,0:T(8,128)S(1)}, f32[192,512]{1,0:T(8,128)S(1)}, u32[]{:S(2)}, u32[]{:S(2)}) collective-permute-start(f32[192,512]{1,0:T(8,128)S(1)} %get-tuple-element.17), channel_id=1, source_target_pairs={{1,0},{2,1},{3,2},{4,3},{5,4},{6,5},{7,6},{8,7},{9,8},{10,9},{11,1... | collective-permute-start | bytes 1179656 | tf_op jit(solution)/shard_map/ppermute | solution.py:277
  3.8 3.0 %collective-permute-start = (f32[192,512]{1,0:T(8,128)S(1)}, f32[192,512]{1,0:T(8,128)S(1)}, u32[]{:S(2)}, u32[]{:S(2)}) collective-permute-start(f32[192,512]{1,0:T(8,128)S(1)} %get-tuple-element.18), channel_id=1, source_target_pairs={{0,1},{1,2},{2,3},{3,4},{4,5},{5,6},{6,7},{7,8},{8,9},{9,10},{10,1... | collective-permute-start | bytes 1179656 | tf_op jit(solution)/shard_map/ppermute | solution.py:277
  6.8 0.8 fusion.1
  7.6 5.0 %collective-permute-start.3 = (f32[64,128]{1,0:T(8,128)S(1)}, f32[64,128]{1,0:T(8,128)S(1)}, u32[]{:S(2)}, u32[]{:S(2)}) collective-permute-start(f32[64,128]{1,0:T(8,128)S(1)} %get-tuple-element.19), channel_id=1, source_target_pairs={{1,0},{2,1},{3,2},{4,3},{5,4},{6,5},{7,6},{8,7},{9,8},{10,9},{11,1... | collective-permute-start | bytes 98312 | tf_op jit(solution)/shard_map/ppermute | solution.py:277
  12.6 1.9 collective-permute-start.2
  14.5 1.4 copy.5.off
  15.9 0.0 collective-permute-done.3.v_down
  15.9 0.0 copy-start.6
  15.9 5.3 %collective-permute-done.2.v_up = f32[64,128]{1,0:T(8,128)S(1)} collective-permute-done((f32[64,128]{1,0:T(8,128)S(1)}, f32[64,128]{1,0:T(8,128)S(1)}, u32[]{:S(2)}, u32[]{:S(2)}) %collective-permute-start.2) | collective-permute-done | bytes 32800 | tf_op jit(solution)/shard_map/ppermute | solution.py:277
  21.1 0.0 copy-start.7
  21.1 0.0 collective-permute-done.1.down
  21.1 0.0 copy-start.4
  21.1 0.0 collective-permute-done.up
  21.1 0.0 copy-start.5
  21.1 0.0 copy-done.6
  21.2 0.6 copy-done.7
  21.8 0.1 copy-done.4
  21.9 0.2 copy-done.5
  22.1 10.0 %powers.1 = (f32[512,512]{1,0:T(8,128)}, f32[512,512]{1,0:T(8,128)}, bf16[2,4,512,512]{3,2,1,0:T(8,128)(2,1)}) custom-call(s32[1]{0:T(128)} %bitcast.core, s32[64,1]{1,0:T(8,128)} %copy.5.off, f32[192,512]{1,0:T(8,128)} %copy-done.5, f32[512,512]{1,0:T(8,128)} %mid.1, f32[192,512]{1,0:T(8,128)} %copy-done.4, f32[64,128]{1,0:T(8,128)} %copy-done.7, ...), custom_call_target="tpu_custom_call" | custom-call | tf_op jit(solution)/shard_map/powers/pallas_call | solution.py:212
  32.1 6.9 %collective-permute-start.4 = (f32[512,512]{1,0:T(8,128)}, f32[512,512]{1,0:T(8,128)S(1)}, u32[]{:S(2)}, u32[]{:S(2)}) collective-permute-start(f32[512,512]{1,0:T(8,128)} %get-tuple-element.12), channel_id=1, source_target_pairs={{0,1},{1,0},{2,3},{3,2},{4,5},{5,4},{6,7},{7,6},{8,9},{9,8},{10,11... | collective-permute-start | bytes 3145736 | tf_op jit(solution)/shard_map/ppermute | solution.py:250
  39.0 2.5 %collective-permute-done.4 = f32[512,512]{1,0:T(8,128)S(1)} collective-permute-done((f32[512,512]{1,0:T(8,128)}, f32[512,512]{1,0:T(8,128)S(1)}, u32[]{:S(2)}, u32[]{:S(2)}) %collective-permute-start.4) | collective-permute-done | bytes 1048608 | tf_op jit(solution)/shard_map/ppermute | solution.py:250
  41.5 1.4 add.24
  42.9 19.3 %all_to_all.20 = f32[16,32,512]{2,1,0:T(8,128)S(1)} all-to-all(f32[16,32,512]{2,1,0:T(8,128)S(1)} %bitcast.8), channel_id=1, replica_groups=mesh['z'=8,'y'=4,'x'=4,'c'=2] {'y','x'}, dimensions={0} | all-to-all | bytes 2097152 | tf_op jit(solution)/shard_map/all_to_all | solution.py:258
  62.2 0.1 reduce_sum.18
  62.2 0.1 collective-permute-start.5
  62.3 3.1 %collective-permute-done.5 = f32[32,512]{1,0:T(8,128)S(1)} collective-permute-done((f32[32,512]{1,0:T(8,128)S(1)}, f32[32,512]{1,0:T(8,128)S(1)}, u32[]{:S(2)}, u32[]{:S(2)}) %collective-permute-start.5) | collective-permute-done | bytes 65568 | tf_op jit(solution)/shard_map/ppermute | solution.py:265
  65.4 4.3 %collective-permute-start.6 = (f32[32,512]{1,0:T(8,128)S(1)}, f32[32,512]{1,0:T(8,128)S(1)}, u32[]{:S(2)}, u32[]{:S(2)}) collective-permute-start(f32[32,512]{1,0:T(8,128)S(1)} %add.25), channel_id=1, source_target_pairs={{0,64},{32,96},{64,0},{96,32},{128,192},{160,224},{192,128},{224,1... | collective-permute-start | bytes 196616 | tf_op jit(solution)/shard_map/ppermute | solution.py:265
  69.7 1.7 collective-permute-done.6
  71.4 5.1 %collective-permute-start.7 = (f32[32,512]{1,0:T(8,128)S(1)}, f32[32,512]{1,0:T(8,128)S(1)}, u32[]{:S(2)}, u32[]{:S(2)}) collective-permute-start(f32[32,512]{1,0:T(8,128)S(1)} %add.26), channel_id=1, source_target_pairs={{0,224},{32,192},{64,160},{96,128},{128,96},{160,64},{192,32},{224... | collective-permute-start | bytes 196616 | tf_op jit(solution)/shard_map/ppermute | solution.py:265
  76.4 2.3 %collective-permute-done.7 = f32[32,512]{1,0:T(8,128)S(1)} collective-permute-done((f32[32,512]{1,0:T(8,128)S(1)}, f32[32,512]{1,0:T(8,128)S(1)}, u32[]{:S(2)}, u32[]{:S(2)}) %collective-permute-start.7) | collective-permute-done | bytes 65568 | tf_op jit(solution)/shard_map/ppermute | solution.py:265
  78.7 0.1 broadcast_in_dim.4
  78.8 16.3 %all_to_all.21 = f32[16,32,512]{2,1,0:T(8,128)S(1)} all-to-all(f32[16,32,512]{2,1,0:T(8,128)S(1)} %broadcast_in_dim.4), channel_id=1, replica_groups=mesh['z'=8,'y'=4,'x'=4,'c'=2] {'y','x'}, dimensions={0} | all-to-all | bytes 2097152 | tf_op jit(solution)/shard_map/all_to_all | solution.py:267
  95.1 0.0 copy-start
  95.1 4.8 %collective-permute-start.8 = (f32[512,512]{1,0:T(8,128)S(1)}, f32[512,512]{1,0:T(8,128)S(1)}, u32[]{:S(2)}, u32[]{:S(2)}) collective-permute-start(f32[512,512]{1,0:T(8,128)S(1)} %bitcast.6), channel_id=1, source_target_pairs={{0,1},{1,0},{2,3},{3,2},{4,5},{5,4},{6,7},{7,6},{8,9},{9,8},{10,11... | collective-permute-start | bytes 3145736 | tf_op jit(solution)/shard_map/ppermute | solution.py:250
  99.9 2.3 %collective-permute-done.8.rest = f32[512,512]{1,0:T(8,128)S(1)} collective-permute-done((f32[512,512]{1,0:T(8,128)S(1)}, f32[512,512]{1,0:T(8,128)S(1)}, u32[]{:S(2)}, u32[]{:S(2)}) %collective-permute-start.8) | collective-permute-done | bytes 1048608 | tf_op jit(solution)/shard_map/ppermute | solution.py:250
  102.2 0.0 copy-start.2
  102.2 0.0 copy-done
  102.2 1.0 copy-done.2
  103.1 33.6 %next_level.1 = (f32[512,512]{1,0:T(8,128)}, f32[512,512]{1,0:T(8,128)}, bf16[2,2,512,512]{3,2,1,0:T(8,128)(2,1)}) custom-call(s32[1]{0:T(128)} %bitcast.core, f32[512,512]{1,0:T(8,128)} %bitcast.7, f32[512,512]{1,0:T(8,128)} %copy-done.2, f32[1024,512]{1,0:T(8,128)} %sketch.3, bf16[2,4,512,512]{3,2,1,0:T(8,128)(2,1)} %get-tuple-element.13.parts), custom_call_target="tpu_custom_call" | custom-call | tf_op jit(solution)/shard_map/next_level/pallas_call | solution.py:227
  136.7 0.4 collective-permute-start.9
  137.1 2.5 %collective-permute-done.9 = f32[512,512]{1,0:T(8,128)S(1)} collective-permute-done((f32[512,512]{1,0:T(8,128)}, f32[512,512]{1,0:T(8,128)S(1)}, u32[]{:S(2)}, u32[]{:S(2)}) %collective-permute-start.9) | collective-permute-done | bytes 1048608 | tf_op jit(solution)/shard_map/ppermute | solution.py:250
  139.6 1.4 add.28
  141.0 19.0 %all_to_all.22 = f32[16,32,512]{2,1,0:T(8,128)S(1)} all-to-all(f32[16,32,512]{2,1,0:T(8,128)S(1)} %bitcast.9), channel_id=1, replica_groups=mesh['z'=8,'y'=4,'x'=4,'c'=2] {'y','x'}, dimensions={0} | all-to-all | bytes 2097152 | tf_op jit(solution)/shard_map/all_to_all | solution.py:258
  160.0 0.1 reduce_sum.19
  160.1 0.3 collective-permute-start.10
  160.4 3.1 %collective-permute-done.10 = f32[32,512]{1,0:T(8,128)S(1)} collective-permute-done((f32[32,512]{1,0:T(8,128)S(1)}, f32[32,512]{1,0:T(8,128)S(1)}, u32[]{:S(2)}, u32[]{:S(2)}) %collective-permute-start.10) | collective-permute-done | bytes 65568 | tf_op jit(solution)/shard_map/ppermute | solution.py:265
  163.5 1.8 collective-permute-start.11
  165.3 2.3 %collective-permute-done.11 = f32[32,512]{1,0:T(8,128)S(1)} collective-permute-done((f32[32,512]{1,0:T(8,128)S(1)}, f32[32,512]{1,0:T(8,128)S(1)}, u32[]{:S(2)}, u32[]{:S(2)}) %collective-permute-start.11) | collective-permute-done | bytes 65568 | tf_op jit(solution)/shard_map/ppermute | solution.py:265
  167.6 4.2 %collective-permute-start.12 = (f32[32,512]{1,0:T(8,128)S(1)}, f32[32,512]{1,0:T(8,128)S(1)}, u32[]{:S(2)}, u32[]{:S(2)}) collective-permute-start(f32[32,512]{1,0:T(8,128)S(1)} %add.30), channel_id=1, source_target_pairs={{0,224},{32,192},{64,160},{96,128},{128,96},{160,64},{192,32},{224... | collective-permute-start | bytes 196616 | tf_op jit(solution)/shard_map/ppermute | solution.py:265
  171.8 2.3 %collective-permute-done.12 = f32[32,512]{1,0:T(8,128)S(1)} collective-permute-done((f32[32,512]{1,0:T(8,128)S(1)}, f32[32,512]{1,0:T(8,128)S(1)}, u32[]{:S(2)}, u32[]{:S(2)}) %collective-permute-start.12) | collective-permute-done | bytes 65568 | tf_op jit(solution)/shard_map/ppermute | solution.py:265
  174.1 0.1 broadcast_in_dim.5
  174.2 15.6 %all_to_all.23 = f32[16,32,512]{2,1,0:T(8,128)S(1)} all-to-all(f32[16,32,512]{2,1,0:T(8,128)S(1)} %broadcast_in_dim.5), channel_id=1, replica_groups=mesh['z'=8,'y'=4,'x'=4,'c'=2] {'y','x'}, dimensions={0} | all-to-all | bytes 2097152 | tf_op jit(solution)/shard_map/all_to_all | solution.py:267
  189.8 0.0 copy-start.1
  189.8 5.6 %collective-permute-start.13 = (f32[512,512]{1,0:T(8,128)S(1)}, f32[512,512]{1,0:T(8,128)S(1)}, u32[]{:S(2)}, u32[]{:S(2)}) collective-permute-start(f32[512,512]{1,0:T(8,128)S(1)} %bitcast.10), channel_id=1, source_target_pairs={{0,1},{1,0},{2,3},{3,2},{4,5},{5,4},{6,7},{7,6},{8,9},{9,8},{10,11... | collective-permute-start | bytes 3145736 | tf_op jit(solution)/shard_map/ppermute | solution.py:250
  195.4 2.3 %collective-permute-done.13.rest = f32[512,512]{1,0:T(8,128)S(1)} collective-permute-done((f32[512,512]{1,0:T(8,128)S(1)}, f32[512,512]{1,0:T(8,128)S(1)}, u32[]{:S(2)}, u32[]{:S(2)}) %collective-permute-start.13) | collective-permute-done | bytes 1048608 | tf_op jit(solution)/shard_map/ppermute | solution.py:250
  197.7 0.0 copy-start.3
  197.7 0.0 copy-done.1
  197.7 1.0 copy-done.3
  198.7 25.8 %last_level.1 = f32[512,512]{1,0:T(8,128)} custom-call(s32[1]{0:T(128)} %bitcast.core, f32[512,512]{1,0:T(8,128)} %bitcast.11, f32[512,512]{1,0:T(8,128)} %copy-done.3, bf16[2,2,512,512]{3,2,1,0:T(8,128)(2,1)} %get-tuple-element.16.parts), custom_call_target="tpu_custom_call" | custom-call | tf_op jit(solution)/shard_map/last_level/pallas_call | solution.py:239
  (6 shorter events, 0.1 us)
Async XLA Ops:
  1.2 20.0 %collective-permute-start.1 = (f32[192,512]{1,0:T(8,128)S(1)}, f32[192,512]{1,0:T(8,128)S(1)}, u32[]{:S(2)}, u32[]{:S(2)}) collective-permute-start(f32[192,512]{1,0:T(8,128)S(1)} %get-tuple-element.17), channel_id=1, source_target_pairs={{1,0},{2,1},{3,2},{4,3},{5,4},{6,5},{7,6},{8,7},{9,8},{10,9},{11,1... | collective-permute-start | bytes 1179656 | tf_op jit(solution)/shard_map/ppermute | solution.py:277
  3.8 17.4 %collective-permute-start = (f32[192,512]{1,0:T(8,128)S(1)}, f32[192,512]{1,0:T(8,128)S(1)}, u32[]{:S(2)}, u32[]{:S(2)}) collective-permute-start(f32[192,512]{1,0:T(8,128)S(1)} %get-tuple-element.18), channel_id=1, source_target_pairs={{0,1},{1,2},{2,3},{3,4},{4,5},{5,6},{6,7},{7,8},{8,9},{9,10},{10,1... | collective-permute-start | bytes 1179656 | tf_op jit(solution)/shard_map/ppermute | solution.py:277
  7.6 8.3 %collective-permute-start.3 = (f32[64,128]{1,0:T(8,128)S(1)}, f32[64,128]{1,0:T(8,128)S(1)}, u32[]{:S(2)}, u32[]{:S(2)}) collective-permute-start(f32[64,128]{1,0:T(8,128)S(1)} %get-tuple-element.19), channel_id=1, source_target_pairs={{1,0},{2,1},{3,2},{4,3},{5,4},{6,5},{7,6},{8,7},{9,8},{10,9},{11,1... | collective-permute-start | bytes 98312 | tf_op jit(solution)/shard_map/ppermute | solution.py:277
  12.6 8.6 %collective-permute-start.2 = (f32[64,128]{1,0:T(8,128)S(1)}, f32[64,128]{1,0:T(8,128)S(1)}, u32[]{:S(2)}, u32[]{:S(2)}) collective-permute-start(f32[64,128]{1,0:T(8,128)S(1)} %get-tuple-element.20), channel_id=1, source_target_pairs={{0,1},{1,2},{2,3},{3,4},{4,5},{5,6},{6,7},{7,8},{8,9},{9,10},{10,1... | collective-permute-start | bytes 98312 | tf_op jit(solution)/shard_map/ppermute | solution.py:277
  15.9 5.3 %copy-start.6 = (f32[64,128]{1,0:T(8,128)}, f32[64,128]{1,0:T(8,128)S(1)}, u32[]{:S(2)}) copy-start(f32[64,128]{1,0:T(8,128)S(1)} %collective-permute-done.3.v_down) | copy-start | bytes 98308
  21.1 0.6 copy-start.7
  21.1 0.8 copy-start.4
  21.1 0.9 copy-start.5
  32.1 9.3 %collective-permute-start.4 = (f32[512,512]{1,0:T(8,128)}, f32[512,512]{1,0:T(8,128)S(1)}, u32[]{:S(2)}, u32[]{:S(2)}) collective-permute-start(f32[512,512]{1,0:T(8,128)} %get-tuple-element.12), channel_id=1, source_target_pairs={{0,1},{1,0},{2,3},{3,2},{4,5},{5,4},{6,7},{7,6},{8,9},{9,8},{10,11... | collective-permute-start | bytes 3145736 | tf_op jit(solution)/shard_map/ppermute | solution.py:250
  62.2 3.2 %collective-permute-start.5 = (f32[32,512]{1,0:T(8,128)S(1)}, f32[32,512]{1,0:T(8,128)S(1)}, u32[]{:S(2)}, u32[]{:S(2)}) collective-permute-start(f32[32,512]{1,0:T(8,128)S(1)} %reduce_sum.18), channel_id=1, source_target_pairs={{0,32},{32,0},{64,96},{96,64},{128,160},{160,128},{192,224},{224,1... | collective-permute-start | bytes 196616 | tf_op jit(solution)/shard_map/ppermute | solution.py:265
  65.4 5.9 %collective-permute-start.6 = (f32[32,512]{1,0:T(8,128)S(1)}, f32[32,512]{1,0:T(8,128)S(1)}, u32[]{:S(2)}, u32[]{:S(2)}) collective-permute-start(f32[32,512]{1,0:T(8,128)S(1)} %add.25), channel_id=1, source_target_pairs={{0,64},{32,96},{64,0},{96,32},{128,192},{160,224},{192,128},{224,1... | collective-permute-start | bytes 196616 | tf_op jit(solution)/shard_map/ppermute | solution.py:265
  71.4 7.3 %collective-permute-start.7 = (f32[32,512]{1,0:T(8,128)S(1)}, f32[32,512]{1,0:T(8,128)S(1)}, u32[]{:S(2)}, u32[]{:S(2)}) collective-permute-start(f32[32,512]{1,0:T(8,128)S(1)} %add.26), channel_id=1, source_target_pairs={{0,224},{32,192},{64,160},{96,128},{128,96},{160,64},{192,32},{224... | collective-permute-start | bytes 196616 | tf_op jit(solution)/shard_map/ppermute | solution.py:265
  95.1 7.1 %copy-start = (f32[16,32,512]{2,1,0:T(8,128)}, f32[16,32,512]{2,1,0:T(8,128)S(1)}, u32[]{:S(2)}) copy-start(f32[16,32,512]{2,1,0:T(8,128)S(1)} %all_to_all.21) | copy-start | bytes 3145732
  95.1 7.0 %collective-permute-start.8 = (f32[512,512]{1,0:T(8,128)S(1)}, f32[512,512]{1,0:T(8,128)S(1)}, u32[]{:S(2)}, u32[]{:S(2)}) collective-permute-start(f32[512,512]{1,0:T(8,128)S(1)} %bitcast.6), channel_id=1, source_target_pairs={{0,1},{1,0},{2,3},{3,2},{4,5},{5,4},{6,7},{7,6},{8,9},{9,8},{10,11... | collective-permute-start | bytes 3145736 | tf_op jit(solution)/shard_map/ppermute | solution.py:250
  102.2 1.0 copy-start.2
  136.7 2.9 %collective-permute-start.9 = (f32[512,512]{1,0:T(8,128)}, f32[512,512]{1,0:T(8,128)S(1)}, u32[]{:S(2)}, u32[]{:S(2)}) collective-permute-start(f32[512,512]{1,0:T(8,128)} %get-tuple-element.15), channel_id=1, source_target_pairs={{0,1},{1,0},{2,3},{3,2},{4,5},{5,4},{6,7},{7,6},{8,9},{9,8},{10,11... | collective-permute-start | bytes 3145736 | tf_op jit(solution)/shard_map/ppermute | solution.py:250
  160.1 3.4 %collective-permute-start.10 = (f32[32,512]{1,0:T(8,128)S(1)}, f32[32,512]{1,0:T(8,128)S(1)}, u32[]{:S(2)}, u32[]{:S(2)}) collective-permute-start(f32[32,512]{1,0:T(8,128)S(1)} %reduce_sum.19), channel_id=1, source_target_pairs={{0,32},{32,0},{64,96},{96,64},{128,160},{160,128},{192,224},{224,1... | collective-permute-start | bytes 196616 | tf_op jit(solution)/shard_map/ppermute | solution.py:265
  163.5 4.1 %collective-permute-start.11 = (f32[32,512]{1,0:T(8,128)S(1)}, f32[32,512]{1,0:T(8,128)S(1)}, u32[]{:S(2)}, u32[]{:S(2)}) collective-permute-start(f32[32,512]{1,0:T(8,128)S(1)} %add.29), channel_id=1, source_target_pairs={{0,64},{32,96},{64,0},{96,32},{128,192},{160,224},{192,128},{224,1... | collective-permute-start | bytes 196616 | tf_op jit(solution)/shard_map/ppermute | solution.py:265
  167.6 6.4 %collective-permute-start.12 = (f32[32,512]{1,0:T(8,128)S(1)}, f32[32,512]{1,0:T(8,128)S(1)}, u32[]{:S(2)}, u32[]{:S(2)}) collective-permute-start(f32[32,512]{1,0:T(8,128)S(1)} %add.30), channel_id=1, source_target_pairs={{0,224},{32,192},{64,160},{96,128},{128,96},{160,64},{192,32},{224... | collective-permute-start | bytes 196616 | tf_op jit(solution)/shard_map/ppermute | solution.py:265
  189.8 7.9 %copy-start.1 = (f32[16,32,512]{2,1,0:T(8,128)}, f32[16,32,512]{2,1,0:T(8,128)S(1)}, u32[]{:S(2)}) copy-start(f32[16,32,512]{2,1,0:T(8,128)S(1)} %all_to_all.23) | copy-start | bytes 3145732
  189.8 7.9 %collective-permute-start.13 = (f32[512,512]{1,0:T(8,128)S(1)}, f32[512,512]{1,0:T(8,128)S(1)}, u32[]{:S(2)}, u32[]{:S(2)}) collective-permute-start(f32[512,512]{1,0:T(8,128)S(1)} %bitcast.10), channel_id=1, source_target_pairs={{0,1},{1,0},{2,3},{3,2},{4,5},{5,4},{6,7},{7,6},{8,9},{9,8},{10,11... | collective-permute-start | bytes 3145736 | tf_op jit(solution)/shard_map/ppermute | solution.py:250
  197.7 1.0 copy-start.3
where the time goes:
time: 225 us; the launch traced here: 224 us
  blocking collectives  70.1 us (31%)
  Pallas kernels  69.4 us (31%)
  starting transfers between devices  45.8 us (20%)
  waiting for transfers between devices  29.5 us (13%)
  local copies, waits for them, and re-layouts  6.42 us (3%)
  other arithmetic  3.07 us (1%)
    all_to_all x2, blocking collectives, sum_over_rows(): part = lax.all_to_all(blocks, ('y', 'x'), 0, 0, tiled=True).sum(0)  38.3 us
    pallas_call x1, Pallas kernels, next_level(): pl.pallas_call(next_body, out_shape=(shaped(width, width), shaped(width,...  33.6 us
    all_to_all x2, blocking collectives, sum_over_rows(): lax.all_to_all(copies, ('y', 'x'), 0, 0, tiled=True).reshape(rows, width)  31.9 us
    pallas_call x1, Pallas kernels, last_level(): pl.pallas_call(last_body, out_shape=shaped(size, width), in_specs=[SMEM]...  25.8 us
    ppermute x4, starting transfers between devices, swap_cores(): return lax.ppermute(x, 'c', [(0, 1), (1, 0)])  17.6 us
    ppermute x6, starting transfers between devices, sum_over_rows(): part = part + lax.ppermute(part, 'z', pairs)  15.7 us
    ppermute x6, waiting for transfers between devices, sum_over_rows(): part = part + lax.ppermute(part, 'z', pairs)  14.7 us
    ppermute x4, starting transfers between devices, from_neighbours(): return (lax.ppermute(last, ROWS, up), lax.ppermute(first, ROWS, down))  12.5 us
  transfers between devices with their start and end apart: 14, of which 11 were waited for; matrix products, arithmetic and copies ran while one was open for 1% of the time, Pallas kernels for 0%

commit v1 on v0

--- a/solution.py
+++ b/solution.py
@@ -14,6 +14,7 @@
 PANEL = 16
 VMEM = pl.BlockSpec(memory_space=pltpu.VMEM)
 SMEM = pl.BlockSpec(memory_space=pltpu.SMEM)
+PARAMS = pltpu.CompilerParams(vmem_limit_bytes=30 * 2**20)
 
 
 def split2(x):
@@ -48,38 +49,62 @@
 def factor_block(d_block):
     n = d_block.shape[0]
     count = n // PANEL
-    row_ids = lax.broadcasted_iota(jnp.int32, (n, n), 0)
-    eye = (row_ids == lax.broadcasted_iota(jnp.int32, (n, n), 1)).astype(F32)
-    both = jnp.concatenate([d_block, eye], 1)
-    panels = [both[PANEL * q : PANEL * (q + 1)] for q in range(count)]
-    sub = lax.broadcasted_iota(jnp.int32, (PANEL, n), 0)
+    rows = [d_block[i : i + 8] for i in range(0, n, 8)]
+    sub = lax.broadcasted_iota(jnp.int32, (8, n), 0)
+    lane = lax.broadcasted_iota(jnp.int32, (8, n), 1)
+    spread = lambda x, r: jnp.broadcast_to(x[r % 8 : r % 8 + 1], (8, n))
+    lanes = lambda x, at: jnp.broadcast_to(x[:, at : at + 1], (8, n))
+    both = range(2)
     inverse = []
     for p in range(count):
-        a, b = panels[p][:, :n], panels[p][:, n:]
         at = PANEL * p
-        cols = [jnp.broadcast_to(a[:, at + j : at + j + 1], (PANEL, n)) for j in range(PANEL)]
-        w = jnp.zeros((PANEL, n), F32)
+        ours = (lane >= at) & (lane < at + PANEL)
+        a = rows[2 * p : 2 * p + 2]
+        cols = [[lanes(a[h], at + j) for h in both] for j in range(PANEL)]
+        if p + 1 < count:
+            below = [[lanes(rows[2 * p + 2 + h], at + j) for h in both] for j in range(PANEL)]
+        left = rows[2 * p + 4 :]
+        a = [jnp.where(ours, (lane == sub + (at + 8 * h)).astype(F32), a[h]) for h in both]
+        w = [jnp.zeros((8, n), F32)] * 2
+        scale = [jnp.zeros((8, n), F32)] * 2
+        d = spread(cols[0][0], 0)
         for k in range(PANEL):
-            m = cols[k]
-            root = lax.rsqrt(m[k : k + 1])
+            g = k // 8
+            here = sub == k % 8
+            root = lax.rsqrt(d)
             inv = root * root
-            keep = sub == k
-            w = jnp.where(keep, b[k : k + 1] * root, w)
-            a = jnp.where(keep, a[k : k + 1] * inv, a - m * (a[k : k + 1] * inv))
-            b = jnp.where(keep, b[k : k + 1] * inv, b - m * (b[k : k + 1] * inv))
+            m = list(cols[k])
+            if k + 1 < PANEL:
+                e = (k + 1) // 8
+                cross = spread(m[e], k + 1) * spread(cols[k + 1][g], k)
+                d = spread(cols[k + 1][e], k + 1) - cross * inv
+            m[g] = jnp.where(here, 0.0, m[g])
+            m = [m[h] * inv for h in both]
+            row = spread(a[g], k)
+            w[g] = jnp.where(here, row * root, w[g])
+            scale[g] = jnp.where(here, inv, scale[g])
+            a = [a[h] - m[h] * row for h in both]
             for j in range(k + 1, PANEL):
-                c = cols[j][k : k + 1] * inv
-                cols[j] = jnp.where(keep, c, cols[j] - m * c)
-        inverse.append(w)
+                c = spread(cols[j][g], k)
+                cols[j] = [cols[j][h] - m[h] * c for h in both]
+        inverse += w
         if p + 1 < count:
-            parts = [jnp.zeros((at, 2 * n), F32)] if p else []
-            parts += [jnp.concatenate([a, b], 1), jnp.zeros((n - at - PANEL, 2 * n), F32)]
-            left = jnp.concatenate([panels[q][:, :n] for q in range(p + 1, count)], 0)
-            change = exact_dot(left, jnp.concatenate(parts, 0))
-            for q in range(p + 1, count):
-                i = PANEL * (q - p - 1)
-                panels[q] = panels[q] - change[i : i + PANEL]
-    return jnp.concatenate(inverse, 0)
+            a = [a[h] * scale[h] for h in both]
+            wide = [spread(a[j // 8], j) for j in range(PANEL)]
+            for h in both:
+                r = 2 * p + 2 + h
+                terms = [below[j][h] * wide[j] for j in range(PANEL)]
+                while len(terms) > 1:
+                    terms = [x + y for x, y in zip(terms[::2], terms[1::2])]
+                rows[r] = jnp.where(ours, 0.0, rows[r]) - terms[0]
+        if p + 2 < count:
+            parts = ([jnp.zeros((at, n), F32)] if p else []) + a + [jnp.zeros((n - at - PANEL, n), F32)]
+            change = exact_dot(jnp.concatenate(left, 0), jnp.concatenate(parts, 0))
+            for i, r in enumerate(range(2 * p + 4, n // 8)):
+                rows[r] = jnp.where(ours, 0.0, rows[r]) - change[8 * i : 8 * i + 8]
+    inverse = jnp.concatenate(inverse, 0)
+    row_ids = lax.broadcasted_iota(jnp.int32, (n, n), 0)
+    return jnp.where(lax.broadcasted_iota(jnp.int32, (n, n), 1) <= row_ids, inverse, 0.0)
 
 
 def invert_factor(work_ref, row_ref, inv_ref):
@@ -123,34 +148,45 @@
         work_ref[at : at + BLOCK, at:] = total
 
 
-def powers_body(core, off, up, mid, down, v_up, v_mid, v_down, sketch, mine, other, parts, dense, long_ref):
+def powers_body(core, off, near, far, mid, v_mid, sketch, mine, other, parts, dense, long_ref):
     n = BLOCK
     size = mid.shape[0]
     width = mid.shape[1]
-    lanes = lax.broadcasted_iota(jnp.int32, (off.shape[0], 2 * n), 1)
-    hot = (off[...] + HALF == lanes).astype(BF16)
+    reach = 3 * HALF
+    blocks = size // n + 2
+    c = core[0]
+    sides = ((near, 1 - c), (far, c))
+    sub = lax.broadcasted_iota(jnp.int32, (8, 2 * n), 0)
+    lanes = lax.broadcasted_iota(jnp.int32, (8, 2 * n), 1)
+    hot = []
+    for g in range(0, off.shape[0], 8):
+        at = jnp.zeros((8, 2 * n), jnp.int32)
+        for r in range(8):
+            at = jnp.where(sub == r, off[g + r], at)
+        hot.append((at + HALF == lanes).astype(F32))
+    hot = jnp.concatenate(hot, 0).astype(BF16)
     hot = jnp.concatenate([hot, hot], 0)
-    blocks = size // n + 2
-    for i in range(blocks):
-        if i == 0:
-            v = v_up[...]
-        elif i == blocks - 1:
-            v = v_down[...]
-        else:
-            v = v_mid[:, n * (i - 1) : n * i]
-        spread = mul(jnp.concatenate(split2(v), 0), hot, (0, 0))
-        spread = pltpu.roll(spread, 0, 1, stride=1, stride_axis=0)
-        dense[0, i], dense[1, i] = split2(spread)
-    reach = 3 * HALF
-    for half, (a, b, c) in enumerate(zip(split2(up[...]), split2(mid[...]), split2(down[...]))):
-        long_ref[half, 0, :reach] = a
+
+    def spread(v, i):
+        block = mul(jnp.concatenate(split2(v), 0), hot, (0, 0))
+        block = pltpu.roll(block, 0, 1, stride=1, stride_axis=0)
+        dense[0, i], dense[1, i] = split2(block)
+
+    for i in range(1, blocks - 1):
+        spread(v_mid[:, n * (i - 1) : n * i], i)
+    for half, b in enumerate(split2(mid[...])):
         long_ref[half, 0, reach : reach + size] = b
-        long_ref[half, 0, reach + size :] = c
         parts[half, 0] = b
         edge = jnp.zeros((HALF, width), BF16)
         for level in (1, 2):
             long_ref[half, level, :HALF] = edge
             long_ref[half, level, size + 2 * reach - HALF :] = edge
+    for side, below in sides:
+        at = pl.multiple_of(below * (reach + size), HALF)
+        for i in range(width // n):
+            for half, b in enumerate(split2(side[reach * i : reach * (i + 1)])):
+                long_ref[half, 0, pl.ds(at, reach), n * i : n * (i + 1)] = b
+        spread(side[reach * (width // n) :], below * (blocks - 1))
     for level in range(3):
         for i in range(blocks) if level < 2 else range(1, blocks - 1):
             window = [long_ref[half, level, n * i : n * i + 2 * n] for half in range(2)]
@@ -207,19 +243,20 @@
     ]
 
 
-def powers(core, off, up, mid, down, v_up, v_mid, v_down, sketch):
+def powers(core, off, near, far, mid, v_mid, sketch):
     size, width = mid.shape
     return pl.pallas_call(
         powers_body,
         out_shape=(shaped(width, width), shaped(width, width), shaped(2, 4, size, width, dtype=BF16)),
-        in_specs=[SMEM] + [VMEM] * 8,
+        in_specs=[SMEM] * 2 + [VMEM] * 5,
         out_specs=(VMEM,) * 3,
         scratch_shapes=[
             pltpu.VMEM((2, size // BLOCK + 2, BLOCK, 2 * BLOCK), BF16),
             pltpu.VMEM((2, 3, size + 6 * HALF, width), BF16),
         ],
+        compiler_params=PARAMS,
         name="powers",
-    )(core, off, up, mid, down, v_up, v_mid, v_down, sketch)
+    )(core, off, near, far, mid, v_mid, sketch)
 
 
 def next_level(core, own, rest, sketch, parts):
@@ -230,6 +267,7 @@
         in_specs=[SMEM] + [VMEM] * 4,
         out_specs=(VMEM,) * 3,
         scratch_shapes=inverse_scratch(width),
+        compiler_params=PARAMS,
         name="next_level",
     )(core, own, rest, sketch, parts)
 
@@ -242,6 +280,7 @@
         in_specs=[SMEM] + [VMEM] * 3,
         out_specs=VMEM,
         scratch_shapes=inverse_scratch(width),
+        compiler_params=PARAMS,
         name="last_level",
     )(core, own, rest, parts)
 
@@ -268,22 +307,26 @@
     return own, swap_cores(own)
 
 
-def from_neighbours(shard, dim, width):
-    size, length = (lax.axis_size(ROWS), shard.shape[dim])
-    up = [(i, i + 1) for i in range(size - 1)]
-    down = [(j, i) for i, j in up]
-    last = lax.slice_in_dim(shard, length - width, length, axis=dim)
-    first = lax.slice_in_dim(shard, 0, width, axis=dim)
-    return lax.ppermute(last, ROWS, up), lax.ppermute(first, ROWS, down)
+def from_neighbours(factor, vals):
+    core = lax.axis_index("c")
+    reach, edge = 3 * HALF, 2 * HALF
+
+    def packed(high):
+        rows = lax.dynamic_slice_in_dim(factor, high * (factor.shape[0] - reach), reach, 0)
+        cols = lax.dynamic_slice_in_dim(vals, high * (vals.shape[1] - edge), edge, 1)
+        return jnp.concatenate([*jnp.split(rows, rows.shape[1] // edge, 1), cols], 0)
+
+    size = lax.axis_size(ROWS)
+    pairs = [(i, i + 1) for i in range(1, size - 1, 2)]
+    pairs += [(j, i) for i, j in pairs]
+    far = lax.ppermute(packed(core), ROWS, pairs)
+    return swap_cores(packed(1 - core)), far
 
 
 def per_device(factor_b, band_vals, offsets, sketch):
     core = lax.axis_index("c").reshape(1)
-    up, down = from_neighbours(factor_b, 0, 3 * HALF)
-    v_up, v_down = from_neighbours(band_vals, 1, 2 * HALF)
-    mine, other, parts = powers(
-        core, offsets.reshape(-1, 1), up, factor_b, down, v_up, band_vals, v_down, sketch
-    )
+    near, far = from_neighbours(factor_b, band_vals)
+    mine, other, parts = powers(core, offsets, near, far, factor_b, band_vals, sketch)
     own, rest = sum_over_rows(mine, other)
     mine, other, parts = next_level(core, own, rest, sketch, parts)
     own, rest = sum_over_rows(mine, other)

time: 225 us -> 203 us (0.902)
  Pallas kernels: 69.4 us -> 51.2 us
  starting transfers between devices: 45.8 us -> 36.9 us
  local copies, waits for them, and re-layouts: 6.42 us -> 13.1 us
  blocking collectives: 70.1 us -> 73.2 us
  waiting for transfers between devices: 29.5 us -> 27 us
  other arithmetic: 3.07 us -> 0.62 us
    unnamed x16 -> x19, local copies, waits for them, and re-layouts: 2.88 us -> 12.1 us
    ppermute x4 -> x1, starting transfers between devices: 12.5 us -> 3.67 us  [from_neighbours(): far = lax.ppermute(packed(core), ROWS, pairs)]
    pallas_call x1, Pallas kernels: 33.6 us -> 24.7 us  [next_level(): pl.pallas_call(next_body, out_shape=(shaped(width, width), shaped(width,...]
    pallas_call x1, Pallas kernels: 25.8 us -> 19.8 us  [last_level(): pl.pallas_call(last_body, out_shape=shaped(size, width), in_specs=[SMEM]...]
    pallas_call x1, Pallas kernels: 10 us -> 6.59 us  [powers(): pl.pallas_call(powers_body, out_shape=(shaped(width, width), shaped(width...]
    all_to_all x2, blocking collectives: 38.3 us -> 41.4 us  [sum_over_rows(): part = lax.all_to_all(blocks, ('y', 'x'), 0, 0, tiled=True).sum(0)]
    add x2, other arithmetic: 2.86 us -> 0.42 us  [sum_over_rows(): half = mine + swap_cores(other)]
    ppermute x4 -> x1, waiting for transfers between devices: 5.27 us -> 2.91 us  [from_neighbours(): far = lax.ppermute(packed(core), ROWS, pairs)]
  transfers between devices with their start and end apart: 14 -> 12, of which waited for: 11 -> 11; matrix products, arithmetic and copies ran while one was open for 1% -> 0% of each run, Pallas kernels for 0% -> 0%
where the time goes in v1:
time: 203 us; the launch traced here: 202 us
  blocking collectives  73.2 us (36%)
  Pallas kernels  51.2 us (25%)
  starting transfers between devices  36.9 us (18%)
  waiting for transfers between devices  27 us (13%)
  local copies, waits for them, and re-layouts  13.1 us (6%)
    all_to_all x2, blocking collectives, sum_over_rows(): part = lax.all_to_all(blocks, ('y', 'x'), 0, 0, tiled=True).sum(0)  41.4 us
    all_to_all x2, blocking collectives, sum_over_rows(): lax.all_to_all(copies, ('y', 'x'), 0, 0, tiled=True).reshape(rows, width)  31.8 us
    pallas_call x1, Pallas kernels, next_level(): pl.pallas_call(next_body, out_shape=(shaped(width, width), shaped(width,...  24.7 us
    pallas_call x1, Pallas kernels, last_level(): pl.pallas_call(last_body, out_shape=shaped(size, width), in_specs=[SMEM]...  19.8 us
    ppermute x5, starting transfers between devices, swap_cores(): return lax.ppermute(x, 'c', [(0, 1), (1, 0)])  19 us
    ppermute x6, waiting for transfers between devices, sum_over_rows(): part = part + lax.ppermute(part, 'z', pairs)  14.9 us
    ppermute x6, starting transfers between devices, sum_over_rows(): part = part + lax.ppermute(part, 'z', pairs)  14.2 us
    unnamed x19, local copies, waits for them, and re-layouts  12.1 us
  transfers between devices with their start and end apart: 12, of which 11 were waited for; matrix products, arithmetic and copies ran while one was open for 0% of the time, Pallas kernels for 0%

profile of v1, /device:TPU:33, one launch (start us, length us, event | category | flops | bytes accessed | tf_op | source)
XLA Modules:
  0.0 202.1 jit_solution(5789729909383812236)
XLA Ops:
  0.0 0.0 copy-start.4
  0.0 1.0 dynamic-slice_dynamic-update-slice_fusion.3
  1.0 1.0 dynamic-slice_dynamic-update-slice_fusion.2
  1.9 1.0 dynamic-slice_dynamic-update-slice_fusion.1
  2.9 1.0 dynamic-slice_dynamic-update-slice_fusion
  3.9 0.9 dynamic-slice_dynamic-update-slice_fusion.4
  4.8 0.8 dynamic-slice_dynamic-update-slice_fusion.8
  5.6 3.7 %collective-permute-start.1 = (f32[832,128]{1,0:T(8,128)S(1)}, f32[832,128]{1,0:T(8,128)S(1)}, u32[]{:S(2)}, u32[]{:S(2)}) collective-permute-start(f32[832,128]{1,0:T(8,128)S(1)} %get-tuple-element.23), channel_id=1, source_target_pairs={{1,2},{3,4},{5,6},{7,8},{9,10},{11,12},{13,14},{15,16},{17,18},{19... | collective-permute-start | bytes 1277960 | tf_op jit(solution)/shard_map/ppermute | solution.py:322
  9.3 3.2 %collective-permute-start = (f32[832,128]{1,0:T(8,128)S(1)}, f32[832,128]{1,0:T(8,128)S(1)}, u32[]{:S(2)}, u32[]{:S(2)}) collective-permute-start(f32[832,128]{1,0:T(8,128)S(1)} %get-tuple-element.24), channel_id=1, source_target_pairs={{0,1},{1,0},{2,3},{3,2},{4,5},{5,4},{6,7},{7,6},{8,9},{9,8},{10,11... | collective-permute-start | bytes 1277960 | tf_op jit(solution)/shard_map/ppermute | solution.py:289
  12.4 2.9 %collective-permute-done.1.far = f32[832,128]{1,0:T(8,128)S(1)} collective-permute-done((f32[832,128]{1,0:T(8,128)S(1)}, f32[832,128]{1,0:T(8,128)S(1)}, u32[]{:S(2)}, u32[]{:S(2)}) %collective-permute-start.1) | collective-permute-done | bytes 426016 | tf_op jit(solution)/shard_map/ppermute | solution.py:322
  15.3 0.0 collective-permute-done.near
  15.4 0.0 copy-done.4
  15.4 0.0 copy-start
  15.4 1.6 copy-done
  16.9 0.0 copy-start.5
  17.0 0.9 copy-done.5
  17.9 0.0 copy-start.6
  17.9 0.7 copy-done.6
  18.5 6.6 %powers.1 = (f32[512,512]{1,0:T(8,128)S(1)}, f32[512,512]{1,0:T(8,128)S(1)}, bf16[2,4,512,512]{3,2,1,0:T(8,128)(2,1)S(1)}) custom-call(s32[1]{0:T(128)} %bitcast.core, s32[64]{0:T(128)S(1)} %copy-done.6, f32[832,128]{1,0:T(8,128)S(1)} %collective-permute-done.near, f32[832,128]{1,0:T(8,128)S(1)} %collective-permute-done.1.far, f32[512,512]{1,0:T(8,128)S(1)} %copy-done.4, ...), custom_call_target="tpu_custom_call" | custom-call | tf_op jit(solution)/shard_map/powers/pallas_call | solution.py:248
  25.1 0.0 copy-start.2
  25.1 1.9 copy-done.2
  27.1 4.6 %collective-permute-start.2 = (f32[512,512]{1,0:T(8,128)S(1)}, f32[512,512]{1,0:T(8,128)S(1)}, u32[]{:S(2)}, u32[]{:S(2)}) collective-permute-start(f32[512,512]{1,0:T(8,128)S(1)} %get-tuple-element.12), channel_id=1, source_target_pairs={{0,1},{1,0},{2,3},{3,2},{4,5},{5,4},{6,7},{7,6},{8,9},{9,8},{10,11... | collective-permute-start | bytes 3145736 | tf_op jit(solution)/shard_map/ppermute | solution.py:289
  31.6 2.3 %collective-permute-done.2 = f32[512,512]{1,0:T(8,128)S(1)} collective-permute-done((f32[512,512]{1,0:T(8,128)S(1)}, f32[512,512]{1,0:T(8,128)S(1)}, u32[]{:S(2)}, u32[]{:S(2)}) %collective-permute-start.2) | collective-permute-done | bytes 1048608 | tf_op jit(solution)/shard_map/ppermute | solution.py:289
  33.9 0.2 add.40
  34.1 22.4 %all_to_all.20 = f32[16,32,512]{2,1,0:T(8,128)S(1)} all-to-all(f32[16,32,512]{2,1,0:T(8,128)S(1)} %bitcast.9), channel_id=1, replica_groups=mesh['z'=8,'y'=4,'x'=4,'c'=2] {'y','x'}, dimensions={0} | all-to-all | bytes 2097152 | tf_op jit(solution)/shard_map/all_to_all | solution.py:297
  56.5 0.1 reduce_sum.18
  56.6 0.0 copy-start.1
  56.6 0.1 collective-permute-start.3
  56.7 3.1 %collective-permute-done.3 = f32[32,512]{1,0:T(8,128)S(1)} collective-permute-done((f32[32,512]{1,0:T(8,128)S(1)}, f32[32,512]{1,0:T(8,128)S(1)}, u32[]{:S(2)}, u32[]{:S(2)}) %collective-permute-start.3) | collective-permute-done | bytes 65568 | tf_op jit(solution)/shard_map/ppermute | solution.py:304
  59.8 4.3 %collective-permute-start.4 = (f32[32,512]{1,0:T(8,128)S(1)}, f32[32,512]{1,0:T(8,128)S(1)}, u32[]{:S(2)}, u32[]{:S(2)}) collective-permute-start(f32[32,512]{1,0:T(8,128)S(1)} %add.41), channel_id=1, source_target_pairs={{0,64},{32,96},{64,0},{96,32},{128,192},{160,224},{192,128},{224,1... | collective-permute-start | bytes 196616 | tf_op jit(solution)/shard_map/ppermute | solution.py:304
  64.1 1.7 collective-permute-done.4
  65.8 3.8 %collective-permute-start.5 = (f32[32,512]{1,0:T(8,128)S(1)}, f32[32,512]{1,0:T(8,128)S(1)}, u32[]{:S(2)}, u32[]{:S(2)}) collective-permute-start(f32[32,512]{1,0:T(8,128)S(1)} %add.42), channel_id=1, source_target_pairs={{0,224},{32,192},{64,160},{96,128},{128,96},{160,64},{192,32},{224... | collective-permute-start | bytes 196616 | tf_op jit(solution)/shard_map/ppermute | solution.py:304
  69.6 2.4 %collective-permute-done.5 = f32[32,512]{1,0:T(8,128)S(1)} collective-permute-done((f32[32,512]{1,0:T(8,128)S(1)}, f32[32,512]{1,0:T(8,128)S(1)}, u32[]{:S(2)}, u32[]{:S(2)}) %collective-permute-start.5) | collective-permute-done | bytes 65568 | tf_op jit(solution)/shard_map/ppermute | solution.py:304
  72.0 0.1 broadcast_in_dim.4
  72.1 16.0 %all_to_all.21 = f32[16,32,512]{2,1,0:T(8,128)S(1)} all-to-all(f32[16,32,512]{2,1,0:T(8,128)S(1)} %broadcast_in_dim.4), channel_id=1, replica_groups=mesh['z'=8,'y'=4,'x'=4,'c'=2] {'y','x'}, dimensions={0} | all-to-all | bytes 2097152 | tf_op jit(solution)/shard_map/all_to_all | solution.py:306
  88.1 5.2 %collective-permute-start.6 = (f32[512,512]{1,0:T(8,128)S(1)}, f32[512,512]{1,0:T(8,128)S(1)}, u32[]{:S(2)}, u32[]{:S(2)}) collective-permute-start(f32[512,512]{1,0:T(8,128)S(1)} %bitcast.5), channel_id=1, source_target_pairs={{0,1},{1,0},{2,3},{3,2},{4,5},{5,4},{6,7},{7,6},{8,9},{9,8},{10,11... | collective-permute-start | bytes 3145736 | tf_op jit(solution)/shard_map/ppermute | solution.py:289
  93.3 2.3 %collective-permute-done.6.rest = f32[512,512]{1,0:T(8,128)S(1)} collective-permute-done((f32[512,512]{1,0:T(8,128)S(1)}, f32[512,512]{1,0:T(8,128)S(1)}, u32[]{:S(2)}, u32[]{:S(2)}) %collective-permute-start.6) | collective-permute-done | bytes 1048608 | tf_op jit(solution)/shard_map/ppermute | solution.py:289
  95.6 0.0 copy-done.1
  95.6 0.0 copy-start.3
  95.6 2.2 %copy-done.3 = bf16[2,4,512,512]{3,2,1,0:T(8,128)(2,1)S(1)} copy-done((bf16[2,4,512,512]{3,2,1,0:T(8,128)(2,1)S(1)}, bf16[2,4,512,512]{3,2,1,0:T(8,128)(2,1)}, u32[]{:S(2)}) %copy-start.3) | copy-done | bytes 4194328
  97.8 24.7 %next_level.1 = (f32[512,512]{1,0:T(8,128)S(1)}, f32[512,512]{1,0:T(8,128)S(1)}, bf16[2,2,512,512]{3,2,1,0:T(8,128)(2,1)S(1)}) custom-call(s32[1]{0:T(128)} %bitcast.core, f32[512,512]{1,0:T(8,128)S(1)} %bitcast.6, f32[512,512]{1,0:T(8,128)S(1)} %collective-permute-done.6.rest, f32[1024,512]{1,0:T(8,128)S(1)} %copy-done.1, bf16[2,4,512,512]{3,2,1,0:T(8,128)(2,1)S(1)} %copy-done.3), custom_call_target="tpu_custom_call" | custom-call | tf_op jit(solution)/shard_map/next_level/pallas_call | solution.py:264
  122.6 0.5 collective-permute-start.7
  123.0 2.3 %collective-permute-done.7 = f32[512,512]{1,0:T(8,128)S(1)} collective-permute-done((f32[512,512]{1,0:T(8,128)S(1)}, f32[512,512]{1,0:T(8,128)S(1)}, u32[]{:S(2)}, u32[]{:S(2)}) %collective-permute-start.7) | collective-permute-done | bytes 1048608 | tf_op jit(solution)/shard_map/ppermute | solution.py:289
  125.3 0.2 add.44
  125.5 19.0 %all_to_all.22 = f32[16,32,512]{2,1,0:T(8,128)S(1)} all-to-all(f32[16,32,512]{2,1,0:T(8,128)S(1)} %bitcast.10), channel_id=1, replica_groups=mesh['z'=8,'y'=4,'x'=4,'c'=2] {'y','x'}, dimensions={0} | all-to-all | bytes 2097152 | tf_op jit(solution)/shard_map/all_to_all | solution.py:297
  144.5 0.1 reduce_sum.19
  144.6 0.3 collective-permute-start.8
  144.9 3.1 %collective-permute-done.8 = f32[32,512]{1,0:T(8,128)S(1)} collective-permute-done((f32[32,512]{1,0:T(8,128)S(1)}, f32[32,512]{1,0:T(8,128)S(1)}, u32[]{:S(2)}, u32[]{:S(2)}) %collective-permute-start.8) | collective-permute-done | bytes 65568 | tf_op jit(solution)/shard_map/ppermute | solution.py:304
  148.0 1.8 collective-permute-start.9
  149.8 2.3 %collective-permute-done.9 = f32[32,512]{1,0:T(8,128)S(1)} collective-permute-done((f32[32,512]{1,0:T(8,128)S(1)}, f32[32,512]{1,0:T(8,128)S(1)}, u32[]{:S(2)}, u32[]{:S(2)}) %collective-permute-start.9) | collective-permute-done | bytes 65568 | tf_op jit(solution)/shard_map/ppermute | solution.py:304
  152.2 3.9 %collective-permute-start.10 = (f32[32,512]{1,0:T(8,128)S(1)}, f32[32,512]{1,0:T(8,128)S(1)}, u32[]{:S(2)}, u32[]{:S(2)}) collective-permute-start(f32[32,512]{1,0:T(8,128)S(1)} %add.46), channel_id=1, source_target_pairs={{0,224},{32,192},{64,160},{96,128},{128,96},{160,64},{192,32},{224... | collective-permute-start | bytes 196616 | tf_op jit(solution)/shard_map/ppermute | solution.py:304
  156.1 2.3 %collective-permute-done.10 = f32[32,512]{1,0:T(8,128)S(1)} collective-permute-done((f32[32,512]{1,0:T(8,128)S(1)}, f32[32,512]{1,0:T(8,128)S(1)}, u32[]{:S(2)}, u32[]{:S(2)}) %collective-permute-start.10) | collective-permute-done | bytes 65568 | tf_op jit(solution)/shard_map/ppermute | solution.py:304
  158.4 0.1 broadcast_in_dim.5
  158.5 15.8 %all_to_all.23 = f32[16,32,512]{2,1,0:T(8,128)S(1)} all-to-all(f32[16,32,512]{2,1,0:T(8,128)S(1)} %broadcast_in_dim.5), channel_id=1, replica_groups=mesh['z'=8,'y'=4,'x'=4,'c'=2] {'y','x'}, dimensions={0} | all-to-all | bytes 2097152 | tf_op jit(solution)/shard_map/all_to_all | solution.py:306
  174.3 5.6 %collective-permute-start.11 = (f32[512,512]{1,0:T(8,128)S(1)}, f32[512,512]{1,0:T(8,128)S(1)}, u32[]{:S(2)}, u32[]{:S(2)}) collective-permute-start(f32[512,512]{1,0:T(8,128)S(1)} %bitcast.7), channel_id=1, source_target_pairs={{0,1},{1,0},{2,3},{3,2},{4,5},{5,4},{6,7},{7,6},{8,9},{9,8},{10,11... | collective-permute-start | bytes 3145736 | tf_op jit(solution)/shard_map/ppermute | solution.py:289
  179.9 2.3 %collective-permute-done.11.rest = f32[512,512]{1,0:T(8,128)S(1)} collective-permute-done((f32[512,512]{1,0:T(8,128)S(1)}, f32[512,512]{1,0:T(8,128)S(1)}, u32[]{:S(2)}, u32[]{:S(2)}) %collective-permute-start.11) | collective-permute-done | bytes 1048608 | tf_op jit(solution)/shard_map/ppermute | solution.py:289
  182.2 19.8 %last_level.1 = f32[512,512]{1,0:T(8,128)} custom-call(s32[1]{0:T(128)} %bitcast.core, f32[512,512]{1,0:T(8,128)S(1)} %bitcast.8, f32[512,512]{1,0:T(8,128)S(1)} %collective-permute-done.11.rest, bf16[2,2,512,512]{3,2,1,0:T(8,128)(2,1)S(1)} %get-tuple-element.16.parts), custom_call_target="tpu_custom_call" | custom-call | tf_op jit(solution)/shard_map/last_level/pallas_call | solution.py:277
  (6 shorter events, 0.1 us)
Async XLA Ops:
  0.0 15.4 %copy-start.4 = (f32[512,512]{1,0:T(8,128)S(1)}, f32[512,512]{1,0:T(8,128)}, u32[]{:S(2)}) copy-start(f32[512,512]{1,0:T(8,128)} %mid.1) | copy-start | bytes 3145732
  5.6 9.8 %collective-permute-start.1 = (f32[832,128]{1,0:T(8,128)S(1)}, f32[832,128]{1,0:T(8,128)S(1)}, u32[]{:S(2)}, u32[]{:S(2)}) collective-permute-start(f32[832,128]{1,0:T(8,128)S(1)} %get-tuple-element.23), channel_id=1, source_target_pairs={{1,2},{3,4},{5,6},{7,8},{9,10},{11,12},{13,14},{15,16},{17,18},{19... | collective-permute-start | bytes 1277960 | tf_op jit(solution)/shard_map/ppermute | solution.py:322
  9.3 6.1 %collective-permute-start = (f32[832,128]{1,0:T(8,128)S(1)}, f32[832,128]{1,0:T(8,128)S(1)}, u32[]{:S(2)}, u32[]{:S(2)}) collective-permute-start(f32[832,128]{1,0:T(8,128)S(1)} %get-tuple-element.24), channel_id=1, source_target_pairs={{0,1},{1,0},{2,3},{3,2},{4,5},{5,4},{6,7},{7,6},{8,9},{9,8},{10,11... | collective-permute-start | bytes 1277960 | tf_op jit(solution)/shard_map/ppermute | solution.py:289
  15.4 1.6 copy-start
  16.9 0.9 copy-start.5
  17.9 0.7 copy-start.6
  25.1 2.0 copy-start.2
  27.1 6.9 %collective-permute-start.2 = (f32[512,512]{1,0:T(8,128)S(1)}, f32[512,512]{1,0:T(8,128)S(1)}, u32[]{:S(2)}, u32[]{:S(2)}) collective-permute-start(f32[512,512]{1,0:T(8,128)S(1)} %get-tuple-element.12), channel_id=1, source_target_pairs={{0,1},{1,0},{2,3},{3,2},{4,5},{5,4},{6,7},{7,6},{8,9},{9,8},{10,11... | collective-permute-start | bytes 3145736 | tf_op jit(solution)/shard_map/ppermute | solution.py:289
  56.6 39.0 %copy-start.1 = (f32[1024,512]{1,0:T(8,128)S(1)}, f32[1024,512]{1,0:T(8,128)}, u32[]{:S(2)}) copy-start(f32[1024,512]{1,0:T(8,128)} %sketch.3) | copy-start | bytes 6291460
  56.6 3.2 %collective-permute-start.3 = (f32[32,512]{1,0:T(8,128)S(1)}, f32[32,512]{1,0:T(8,128)S(1)}, u32[]{:S(2)}, u32[]{:S(2)}) collective-permute-start(f32[32,512]{1,0:T(8,128)S(1)} %reduce_sum.18), channel_id=1, source_target_pairs={{0,32},{32,0},{64,96},{96,64},{128,160},{160,128},{192,224},{224,1... | collective-permute-start | bytes 196616 | tf_op jit(solution)/shard_map/ppermute | solution.py:304
  59.8 5.9 %collective-permute-start.4 = (f32[32,512]{1,0:T(8,128)S(1)}, f32[32,512]{1,0:T(8,128)S(1)}, u32[]{:S(2)}, u32[]{:S(2)}) collective-permute-start(f32[32,512]{1,0:T(8,128)S(1)} %add.41), channel_id=1, source_target_pairs={{0,64},{32,96},{64,0},{96,32},{128,192},{160,224},{192,128},{224,1... | collective-permute-start | bytes 196616 | tf_op jit(solution)/shard_map/ppermute | solution.py:304
  65.8 6.2 %collective-permute-start.5 = (f32[32,512]{1,0:T(8,128)S(1)}, f32[32,512]{1,0:T(8,128)S(1)}, u32[]{:S(2)}, u32[]{:S(2)}) collective-permute-start(f32[32,512]{1,0:T(8,128)S(1)} %add.42), channel_id=1, source_target_pairs={{0,224},{32,192},{64,160},{96,128},{128,96},{160,64},{192,32},{224... | collective-permute-start | bytes 196616 | tf_op jit(solution)/shard_map/ppermute | solution.py:304
  88.1 7.5 %collective-permute-start.6 = (f32[512,512]{1,0:T(8,128)S(1)}, f32[512,512]{1,0:T(8,128)S(1)}, u32[]{:S(2)}, u32[]{:S(2)}) collective-permute-start(f32[512,512]{1,0:T(8,128)S(1)} %bitcast.5), channel_id=1, source_target_pairs={{0,1},{1,0},{2,3},{3,2},{4,5},{5,4},{6,7},{7,6},{8,9},{9,8},{10,11... | collective-permute-start | bytes 3145736 | tf_op jit(solution)/shard_map/ppermute | solution.py:289
  95.6 2.2 %copy-start.3 = (bf16[2,4,512,512]{3,2,1,0:T(8,128)(2,1)S(1)}, bf16[2,4,512,512]{3,2,1,0:T(8,128)(2,1)}, u32[]{:S(2)}) copy-start(bf16[2,4,512,512]{3,2,1,0:T(8,128)(2,1)} %copy-done.2) | copy-start | bytes 12582916
  122.6 2.8 %collective-permute-start.7 = (f32[512,512]{1,0:T(8,128)S(1)}, f32[512,512]{1,0:T(8,128)S(1)}, u32[]{:S(2)}, u32[]{:S(2)}) collective-permute-start(f32[512,512]{1,0:T(8,128)S(1)} %get-tuple-element.15), channel_id=1, source_target_pairs={{0,1},{1,0},{2,3},{3,2},{4,5},{5,4},{6,7},{7,6},{8,9},{9,8},{10,11... | collective-permute-start | bytes 3145736 | tf_op jit(solution)/shard_map/ppermute | solution.py:289
  144.6 3.4 %collective-permute-start.8 = (f32[32,512]{1,0:T(8,128)S(1)}, f32[32,512]{1,0:T(8,128)S(1)}, u32[]{:S(2)}, u32[]{:S(2)}) collective-permute-start(f32[32,512]{1,0:T(8,128)S(1)} %reduce_sum.19), channel_id=1, source_target_pairs={{0,32},{32,0},{64,96},{96,64},{128,160},{160,128},{192,224},{224,1... | collective-permute-start | bytes 196616 | tf_op jit(solution)/shard_map/ppermute | solution.py:304
  148.0 4.1 %collective-permute-start.9 = (f32[32,512]{1,0:T(8,128)S(1)}, f32[32,512]{1,0:T(8,128)S(1)}, u32[]{:S(2)}, u32[]{:S(2)}) collective-permute-start(f32[32,512]{1,0:T(8,128)S(1)} %add.45), channel_id=1, source_target_pairs={{0,64},{32,96},{64,0},{96,32},{128,192},{160,224},{192,128},{224,1... | collective-permute-start | bytes 196616 | tf_op jit(solution)/shard_map/ppermute | solution.py:304
  152.2 6.2 %collective-permute-start.10 = (f32[32,512]{1,0:T(8,128)S(1)}, f32[32,512]{1,0:T(8,128)S(1)}, u32[]{:S(2)}, u32[]{:S(2)}) collective-permute-start(f32[32,512]{1,0:T(8,128)S(1)} %add.46), channel_id=1, source_target_pairs={{0,224},{32,192},{64,160},{96,128},{128,96},{160,64},{192,32},{224... | collective-permute-start | bytes 196616 | tf_op jit(solution)/shard_map/ppermute | solution.py:304
  174.3 7.9 %collective-permute-start.11 = (f32[512,512]{1,0:T(8,128)S(1)}, f32[512,512]{1,0:T(8,128)S(1)}, u32[]{:S(2)}, u32[]{:S(2)}) collective-permute-start(f32[512,512]{1,0:T(8,128)S(1)} %bitcast.7), channel_id=1, source_target_pairs={{0,1},{1,0},{2,3},{3,2},{4,5},{5,4},{6,7},{7,6},{8,9},{9,8},{10,11... | collective-permute-start | bytes 3145736 | tf_op jit(solution)/shard_map/ppermute | solution.py:289

commit v2 on v1

--- a/solution.py
+++ b/solution.py
@@ -14,7 +14,8 @@
 PANEL = 16
 VMEM = pl.BlockSpec(memory_space=pltpu.VMEM)
 SMEM = pl.BlockSpec(memory_space=pltpu.SMEM)
-PARAMS = pltpu.CompilerParams(vmem_limit_bytes=30 * 2**20)
+HBM = pl.BlockSpec(memory_space=pltpu.HBM)
+PARAMS = pltpu.CompilerParams(vmem_limit_bytes=40 * 2**20)
 
 
 def split2(x):
@@ -107,14 +108,16 @@
     return jnp.where(lax.broadcasted_iota(jnp.int32, (n, n), 1) <= row_ids, inverse, 0.0)
 
 
-def invert_factor(work_ref, row_ref, inv_ref):
+def invert_factor(work_ref, row_ref, inv_ref, beside):
     n = BLOCK
     count = work_ref.shape[0] // n
     lane = lax.broadcasted_iota(jnp.int32, (n, count * n), 1) // n
 
     def step(b, carry):
         at = pl.multiple_of(b * n, n)
-        w = factor_block(work_ref[pl.ds(at, n), pl.ds(at, n)])
+        d_block = work_ref[pl.ds(at, n), pl.ds(at, n)]
+        beside(b, at)
+        w = factor_block(d_block)
         row = exact_dot(w, work_ref[pl.ds(at, n), :])
         row = jnp.where(lane == b, jnp.concatenate([w] * count, 1), row)
         row_ref[...] = row
@@ -148,13 +151,42 @@
         work_ref[at : at + BLOCK, at:] = total
 
 
-def powers_body(core, off, near, far, mid, v_mid, sketch, mine, other, parts, dense, long_ref):
+def copies(pairs, sems):
+    return [pltpu.make_async_copy(src, dst, sems.at[i]) for i, (src, dst) in enumerate(pairs)]
+
+
+def pack_body(core, mid, v_mid, near, far, sems):
+    c = core[0]
+    edge = 2 * HALF
+    reach = 3 * HALF
+    moves = []
+    for out, high in ((near, 1 - c), (far, c)):
+        at = pl.multiple_of(high * (mid.shape[0] - reach), HALF)
+        count = mid.shape[1] // edge
+        for i in range(count):
+            src = mid.at[pl.ds(at, reach), pl.ds(i * edge, edge)]
+            moves.append((src, out.at[pl.ds(i * reach, reach)]))
+        at = pl.multiple_of(high * (v_mid.shape[1] - edge), edge)
+        moves.append((v_mid.at[:, pl.ds(at, edge)], out.at[pl.ds(count * reach, v_mid.shape[0])]))
+    moves = copies(moves, sems)
+    for move in moves:
+        move.start()
+    for move in moves:
+        move.wait()
+
+
+def powers_body(
+    core, off, near, far, mid_hbm, v_hbm, sketch_hbm, mine, other, parts_hbm, dense, long_ref, mid, v_mid, sketch, parts, sems
+):
     n = BLOCK
     size = mid.shape[0]
     width = mid.shape[1]
     reach = 3 * HALF
     blocks = size // n + 2
     c = core[0]
+    fetch = copies(((v_hbm, v_mid), (mid_hbm, mid), (sketch_hbm, sketch)), sems)
+    for move in fetch:
+        move.start()
     sides = ((near, 1 - c), (far, c))
     sub = lax.broadcasted_iota(jnp.int32, (8, 2 * n), 0)
     lanes = lax.broadcasted_iota(jnp.int32, (8, 2 * n), 1)
@@ -172,8 +204,16 @@
         block = pltpu.roll(block, 0, 1, stride=1, stride_axis=0)
         dense[0, i], dense[1, i] = split2(block)
 
+    for side, below in sides:
+        at = pl.multiple_of(below * (reach + size), HALF)
+        for i in range(width // n):
+            for half, b in enumerate(split2(side[reach * i : reach * (i + 1)])):
+                long_ref[half, 0, pl.ds(at, reach), n * i : n * (i + 1)] = b
+        spread(side[reach * (width // n) :], below * (blocks - 1))
+    fetch[0].wait()
     for i in range(1, blocks - 1):
         spread(v_mid[:, n * (i - 1) : n * i], i)
+    fetch[1].wait()
     for half, b in enumerate(split2(mid[...])):
         long_ref[half, 0, reach : reach + size] = b
         parts[half, 0] = b
@@ -181,12 +221,8 @@
         for level in (1, 2):
             long_ref[half, level, :HALF] = edge
             long_ref[half, level, size + 2 * reach - HALF :] = edge
-    for side, below in sides:
-        at = pl.multiple_of(below * (reach + size), HALF)
-        for i in range(width // n):
-            for half, b in enumerate(split2(side[reach * i : reach * (i + 1)])):
-                long_ref[half, 0, pl.ds(at, reach), n * i : n * (i + 1)] = b
-        spread(side[reach * (width // n) :], below * (blocks - 1))
+    store = copies([(parts.at[:, level], parts_hbm.at[:, level]) for level in range(4)], sems.at[pl.ds(3, 4)])
+    store[0].start()
     for level in range(3):
         for i in range(blocks) if level < 2 else range(1, blocks - 1):
             window = [long_ref[half, level, n * i : n * i + 2 * n] for half in range(2)]
@@ -196,7 +232,11 @@
                     long_ref[half, level + 1, n * i + HALF : n * i + HALF + n] = result[half]
                 if 0 < i < blocks - 1:
                     parts[half, level + 1, n * (i - 1) : n * i] = result[half]
+        store[level + 1].start()
+    fetch[2].wait()
     gram_halves(core, parts, sketch, mine, other)
+    for move in store:
+        move.wait()
 
 
 def gram_halves(core, parts, sketch, mine, other):
@@ -209,50 +249,98 @@
     other[...] = near_dot(get(1 - c), projected, (0, 0))
 
 
-def next_body(core, own, rest, sketch, parts, mine, other, new_parts, work, row, inv):
+def basis_products(core, own, rest, parts, work, row, inv, halves, reached, arrived):
     c = core[0]
     normal_matrix(own[...], rest[...], work)
-    invert_factor(work, row, inv)
-    sides = (split2(own[...]), split2(rest[...]))
+    halves[0, 0], halves[1, 0] = split2(own[...])
+    halves[0, 1], halves[1, 1] = split2(rest[...])
+
+    def beside(b, at):
+        arrived(b)
+        get = lambda s: (parts[0, s, pl.ds(at, BLOCK)], parts[1, s, pl.ds(at, BLOCK)])
+        for s in range(reached.shape[1]):
+            total = near_dot(get(2 * s + c), (halves[0, 0], halves[1, 0]))
+            total += near_dot(get(2 * s + 1 - c), (halves[0, 1], halves[1, 1]))
+            reached[0, s, pl.ds(at, BLOCK)], reached[1, s, pl.ds(at, BLOCK)] = split2(total)
+
+    invert_factor(work, row, inv, beside)
+
+
+def share(src, dst, sems, b):
+    rows = pl.ds(pl.multiple_of(b * BLOCK, BLOCK), BLOCK)
+    return pltpu.make_async_copy(src.at[:, :, rows], dst.at[:, :, rows], sems.at[b])
+
+
+def next_body(
+    core, own, rest, sketch_hbm, parts_hbm, mine, other, new_hbm, work, row, inv, halves, reached, parts, sketch, new_parts, sems
+):
+    blocks = parts.shape[2] // BLOCK
+    for b in range(blocks):
+        share(parts_hbm, parts, sems, b).start()
+    fetch, store = copies(((sketch_hbm, sketch), (new_parts, new_hbm)), sems.at[pl.ds(blocks, 2)])
+    fetch.start()
+    arrived = lambda b: share(parts_hbm, parts, sems, b).wait()
+    basis_products(core, own, rest, parts, work, row, inv, halves, reached, arrived)
     for s in range(2):
-        reached = near_dot((parts[0, 2 * s + c], parts[1, 2 * s + c]), sides[0])
-        reached += near_dot((parts[0, 2 * s + 1 - c], parts[1, 2 * s + 1 - c]), sides[1])
-        result = near_dot(split2(reached), (inv[0], inv[1]), (1, 1))
+        result = near_dot((reached[0, s], reached[1, s]), (inv[0], inv[1]), (1, 1))
         new_parts[0, s], new_parts[1, s] = split2(result)
+    store.start()
+    fetch.wait()
     gram_halves(core, new_parts, sketch, mine, other)
-
-
-def last_body(core, own, rest, parts, out, work, row, inv):
-    c = core[0]
-    normal_matrix(own[...], rest[...], work)
-    invert_factor(work, row, inv)
-    reached = near_dot((parts[0, c], parts[1, c]), split2(own[...]))
-    reached += near_dot((parts[0, 1 - c], parts[1, 1 - c]), split2(rest[...]))
-    out[...] = near_dot(split2(reached), (inv[0], inv[1]), (1, 1))
+    store.wait()
+
+
+def last_body(core, own, rest, parts_hbm, out, work, row, inv, halves, reached, parts, sems):
+    for b in range(parts.shape[2] // BLOCK):
+        share(parts_hbm, parts, sems, b).start()
+    arrived = lambda b: share(parts_hbm, parts, sems, b).wait()
+    basis_products(core, own, rest, parts, work, row, inv, halves, reached, arrived)
+    out[...] = near_dot((reached[0, 0], reached[1, 0]), (inv[0], inv[1]), (1, 1))
 
 
 def shaped(*shape, dtype=F32):
     return jax.ShapeDtypeStruct(shape, dtype)
 
 
-def inverse_scratch(width):
+def inverse_scratch(size, width, count):
     return [
         pltpu.VMEM((width, width), F32),
         pltpu.VMEM((BLOCK, width), F32),
         pltpu.VMEM((2, width, width), BF16),
+        pltpu.VMEM((2, 2, width, width), BF16),
+        pltpu.VMEM((2, count, size, width), BF16),
+        pltpu.VMEM((2, 2 * count, size, width), BF16),
     ]
+
+
+def pack(core, mid, v_mid):
+    shape = shaped(3 * HALF * mid.shape[1] // BLOCK + v_mid.shape[0], BLOCK)
+    return pl.pallas_call(
+        pack_body,
+        out_shape=(shape, shape),
+        in_specs=[SMEM, HBM, HBM],
+        out_specs=(VMEM, VMEM),
+        scratch_shapes=[pltpu.SemaphoreType.DMA((2 * (mid.shape[1] // BLOCK + 1),))],
+        compiler_params=PARAMS,
+        name="pack",
+    )(core, mid, v_mid)
 
 
 def powers(core, off, near, far, mid, v_mid, sketch):
     size, width = mid.shape
     return pl.pallas_call(
         powers_body,
-        out_shape=(shaped(width, width), shaped(width, width), shaped(2, 4, size, width, dtype=BF16)),
-        in_specs=[SMEM] * 2 + [VMEM] * 5,
-        out_specs=(VMEM,) * 3,
+        out_shape=(shaped(width, width), shaped(width, width), pltpu.HBM((2, 4, size, width), BF16)),
+        in_specs=[SMEM] * 2 + [VMEM] * 2 + [HBM] * 3,
+        out_specs=(VMEM, VMEM, HBM),
         scratch_shapes=[
             pltpu.VMEM((2, size // BLOCK + 2, BLOCK, 2 * BLOCK), BF16),
             pltpu.VMEM((2, 3, size + 6 * HALF, width), BF16),
+            pltpu.VMEM(mid.shape, F32),
+            pltpu.VMEM(v_mid.shape, F32),
+            pltpu.VMEM(sketch.shape, F32),
+            pltpu.VMEM((2, 4, size, width), BF16),
+            pltpu.SemaphoreType.DMA((7,)),
         ],
         compiler_params=PARAMS,
         name="powers",
@@ -263,10 +351,15 @@
     size, width = parts.shape[2:]
     return pl.pallas_call(
         next_body,
-        out_shape=(shaped(width, width), shaped(width, width), shaped(2, 2, size, width, dtype=BF16)),
-        in_specs=[SMEM] + [VMEM] * 4,
-        out_specs=(VMEM,) * 3,
-        scratch_shapes=inverse_scratch(width),
+        out_shape=(shaped(width, width), shaped(width, width), pltpu.HBM((2, 2, size, width), BF16)),
+        in_specs=[SMEM] + [VMEM] * 2 + [HBM] * 2,
+        out_specs=(VMEM, VMEM, HBM),
+        scratch_shapes=inverse_scratch(size, width, 2)
+        + [
+            pltpu.VMEM(sketch.shape, F32),
+            pltpu.VMEM((2, 2, size, width), BF16),
+            pltpu.SemaphoreType.DMA((size // BLOCK + 2,)),
+        ],
         compiler_params=PARAMS,
         name="next_level",
     )(core, own, rest, sketch, parts)
@@ -277,9 +370,9 @@
     return pl.pallas_call(
         last_body,
         out_shape=shaped(size, width),
-        in_specs=[SMEM] + [VMEM] * 3,
+        in_specs=[SMEM] + [VMEM] * 2 + [HBM],
         out_specs=VMEM,
-        scratch_shapes=inverse_scratch(width),
+        scratch_shapes=inverse_scratch(size, width, 1) + [pltpu.SemaphoreType.DMA((size // BLOCK,))],
         compiler_params=PARAMS,
         name="last_level",
     )(core, own, rest, parts)
@@ -307,29 +400,23 @@
     return own, swap_cores(own)
 
 
-def from_neighbours(factor, vals):
-    core = lax.axis_index("c")
-    reach, edge = 3 * HALF, 2 * HALF
-
-    def packed(high):
-        rows = lax.dynamic_slice_in_dim(factor, high * (factor.shape[0] - reach), reach, 0)
-        cols = lax.dynamic_slice_in_dim(vals, high * (vals.shape[1] - edge), edge, 1)
-        return jnp.concatenate([*jnp.split(rows, rows.shape[1] // edge, 1), cols], 0)
-
+def swap_chips(x):
     size = lax.axis_size(ROWS)
     pairs = [(i, i + 1) for i in range(1, size - 1, 2)]
-    pairs += [(j, i) for i, j in pairs]
-    far = lax.ppermute(packed(core), ROWS, pairs)
-    return swap_cores(packed(1 - core)), far
+    return lax.ppermute(x, ROWS, pairs + [(j, i) for i, j in pairs])
 
 
 def per_device(factor_b, band_vals, offsets, sketch):
     core = lax.axis_index("c").reshape(1)
-    near, far = from_neighbours(factor_b, band_vals)
+    factor_b, band_vals, sketch = (pltpu.with_memory_space_constraint(x, pltpu.HBM) for x in (factor_b, band_vals, sketch))
+    near, far = pack(core, factor_b, band_vals)
+    near, far = swap_cores(near), swap_chips(far)
     mine, other, parts = powers(core, offsets, near, far, factor_b, band_vals, sketch)
     own, rest = sum_over_rows(mine, other)
+    parts = pltpu.with_memory_space_constraint(parts, pltpu.HBM)
     mine, other, parts = next_level(core, own, rest, sketch, parts)
     own, rest = sum_over_rows(mine, other)
+    parts = pltpu.with_memory_space_constraint(parts, pltpu.HBM)
     return last_level(core, own, rest, parts)
 
 

time: 203 us -> 193 us (0.951)
  local copies, waits for them, and re-layouts: 13.1 us -> 0.89 us
  waiting for transfers between devices: 27 us -> 30.7 us
  starting transfers between devices: 36.9 us -> 33.3 us
    unnamed x19 -> x2, local copies, waits for them, and re-layouts: 12.1 us -> 0.66 us
    ppermute x1, waiting for transfers between devices: 2.91 us -> 6.69 us  [swap_chips(): return lax.ppermute(x, ROWS, pairs + [(j, i) for i, j in pairs])]
    ppermute x5, starting transfers between devices: 19 us -> 16.1 us  [swap_cores(): return lax.ppermute(x, 'c', [(0, 1), (1, 0)])]
where the time goes in v2:
time: 193 us; the launch traced here: 192 us
  blocking collectives  73.9 us (38%)
  Pallas kernels  52.7 us (27%)
  starting transfers between devices  33.3 us (17%)
  waiting for transfers between devices  30.7 us (16%)
    all_to_all x2, blocking collectives, sum_over_rows(): part = lax.all_to_all(blocks, ('y', 'x'), 0, 0, tiled=True).sum(0)  42.1 us
    all_to_all x2, blocking collectives, sum_over_rows(): lax.all_to_all(copies, ('y', 'x'), 0, 0, tiled=True).reshape(rows, width)  31.8 us
    pallas_call x1, Pallas kernels, next_level(): pl.pallas_call(next_body, out_shape=(shaped(width, width), shaped(width,...  24.5 us
    pallas_call x1, Pallas kernels, last_level(): pl.pallas_call(last_body, out_shape=shaped(size, width), in_specs=[SMEM]...  19.5 us
    ppermute x5, starting transfers between devices, swap_cores(): return lax.ppermute(x, 'c', [(0, 1), (1, 0)])  16.1 us
    ppermute x6, waiting for transfers between devices, sum_over_rows(): part = part + lax.ppermute(part, 'z', pairs)  14.9 us
    ppermute x6, starting transfers between devices, sum_over_rows(): part = part + lax.ppermute(part, 'z', pairs)  14.2 us
    ppermute x5, waiting for transfers between devices, swap_cores(): return lax.ppermute(x, 'c', [(0, 1), (1, 0)])  9.15 us
  transfers between devices with their start and end apart: 12, of which 11 were waited for; matrix products, arithmetic and copies ran while one was open for 0% of the time, Pallas kernels for 0%

profile of v2, /device:TPU:33, one launch (start us, length us, event | category | flops | bytes accessed | tf_op | source)
XLA Modules:
  0.0 192.4 jit_solution(11908408047850882696)
XLA Ops:
  0.0 1.3 pack.1
  1.3 0.8 collective-permute-start
  2.1 3.0 %collective-permute-start.1 = (f32[832,128]{1,0:T(8,128)S(1)}, f32[832,128]{1,0:T(8,128)S(1)}, u32[]{:S(2)}, u32[]{:S(2)}) collective-permute-start(f32[832,128]{1,0:T(8,128)S(1)} %get-tuple-element.14), channel_id=1, source_target_pairs={{1,2},{3,4},{5,6},{7,8},{9,10},{11,12},{13,14},{15,16},{17,18},{19... | collective-permute-start | bytes 1277960 | tf_op jit(solution)/shard_map/ppermute | solution.py:406
  5.1 0.0 collective-permute-done.near
  5.1 6.7 %collective-permute-done.1.far = f32[832,128]{1,0:T(8,128)S(1)} collective-permute-done((f32[832,128]{1,0:T(8,128)S(1)}, f32[832,128]{1,0:T(8,128)S(1)}, u32[]{:S(2)}, u32[]{:S(2)}) %collective-permute-start.1) | collective-permute-done | bytes 426016 | tf_op jit(solution)/shard_map/ppermute | solution.py:406
  11.8 0.0 copy-start
  11.8 0.7 copy-done
  12.5 7.4 %powers.1 = (f32[512,512]{1,0:T(8,128)S(1)}, f32[512,512]{1,0:T(8,128)S(1)}, bf16[2,4,512,512]{3,2,1,0:T(8,128)(2,1)}) custom-call(s32[1]{0:T(128)} %bitcast.core, s32[64]{0:T(128)S(1)} %copy-done, f32[832,128]{1,0:T(8,128)S(1)} %collective-permute-done.near, f32[832,128]{1,0:T(8,128)S(1)} %collective-permute-done.1.far, f32[512,512]{1,0:T(8,128)} %mid_hbm.1, ...), custom_call_target="tpu_custom_call" | custom-call | tf_op jit(solution)/shard_map/powers/pallas_call | solution.py:331
  19.8 4.0 %collective-permute-start.2 = (f32[512,512]{1,0:T(8,128)S(1)}, f32[512,512]{1,0:T(8,128)S(1)}, u32[]{:S(2)}, u32[]{:S(2)}) collective-permute-start(f32[512,512]{1,0:T(8,128)S(1)} %get-tuple-element.16), channel_id=1, source_target_pairs={{0,1},{1,0},{2,3},{3,2},{4,5},{5,4},{6,7},{7,6},{8,9},{9,8},{10,11... | collective-permute-start | bytes 3145736 | tf_op jit(solution)/shard_map/ppermute | solution.py:382
  23.9 2.3 %collective-permute-done.2 = f32[512,512]{1,0:T(8,128)S(1)} collective-permute-done((f32[512,512]{1,0:T(8,128)S(1)}, f32[512,512]{1,0:T(8,128)S(1)}, u32[]{:S(2)}, u32[]{:S(2)}) %collective-permute-start.2) | collective-permute-done | bytes 1048608 | tf_op jit(solution)/shard_map/ppermute | solution.py:382
  26.2 0.2 add.24
  26.4 23.0 %all_to_all.20 = f32[16,32,512]{2,1,0:T(8,128)S(1)} all-to-all(f32[16,32,512]{2,1,0:T(8,128)S(1)} %bitcast.9), channel_id=1, replica_groups=mesh['z'=8,'y'=4,'x'=4,'c'=2] {'y','x'}, dimensions={0} | all-to-all | bytes 2097152 | tf_op jit(solution)/shard_map/all_to_all | solution.py:390
  49.4 0.1 reduce_sum.18
  49.5 0.1 collective-permute-start.3
  49.6 3.1 %collective-permute-done.3 = f32[32,512]{1,0:T(8,128)S(1)} collective-permute-done((f32[32,512]{1,0:T(8,128)S(1)}, f32[32,512]{1,0:T(8,128)S(1)}, u32[]{:S(2)}, u32[]{:S(2)}) %collective-permute-start.3) | collective-permute-done | bytes 65568 | tf_op jit(solution)/shard_map/ppermute | solution.py:397
  52.7 4.3 %collective-permute-start.4 = (f32[32,512]{1,0:T(8,128)S(1)}, f32[32,512]{1,0:T(8,128)S(1)}, u32[]{:S(2)}, u32[]{:S(2)}) collective-permute-start(f32[32,512]{1,0:T(8,128)S(1)} %add.25), channel_id=1, source_target_pairs={{0,64},{32,96},{64,0},{96,32},{128,192},{160,224},{192,128},{224,1... | collective-permute-start | bytes 196616 | tf_op jit(solution)/shard_map/ppermute | solution.py:397
  57.0 1.7 collective-permute-done.4
  58.7 3.8 %collective-permute-start.5 = (f32[32,512]{1,0:T(8,128)S(1)}, f32[32,512]{1,0:T(8,128)S(1)}, u32[]{:S(2)}, u32[]{:S(2)}) collective-permute-start(f32[32,512]{1,0:T(8,128)S(1)} %add.26), channel_id=1, source_target_pairs={{0,224},{32,192},{64,160},{96,128},{128,96},{160,64},{192,32},{224... | collective-permute-start | bytes 196616 | tf_op jit(solution)/shard_map/ppermute | solution.py:397
  62.5 2.4 %collective-permute-done.5 = f32[32,512]{1,0:T(8,128)S(1)} collective-permute-done((f32[32,512]{1,0:T(8,128)S(1)}, f32[32,512]{1,0:T(8,128)S(1)}, u32[]{:S(2)}, u32[]{:S(2)}) %collective-permute-start.5) | collective-permute-done | bytes 65568 | tf_op jit(solution)/shard_map/ppermute | solution.py:397
  64.9 0.1 broadcast_in_dim.4
  65.0 16.0 %all_to_all.21 = f32[16,32,512]{2,1,0:T(8,128)S(1)} all-to-all(f32[16,32,512]{2,1,0:T(8,128)S(1)} %broadcast_in_dim.4), channel_id=1, replica_groups=mesh['z'=8,'y'=4,'x'=4,'c'=2] {'y','x'}, dimensions={0} | all-to-all | bytes 2097152 | tf_op jit(solution)/shard_map/all_to_all | solution.py:399
  81.0 5.2 %collective-permute-start.6 = (f32[512,512]{1,0:T(8,128)S(1)}, f32[512,512]{1,0:T(8,128)S(1)}, u32[]{:S(2)}, u32[]{:S(2)}) collective-permute-start(f32[512,512]{1,0:T(8,128)S(1)} %bitcast.5), channel_id=1, source_target_pairs={{0,1},{1,0},{2,3},{3,2},{4,5},{5,4},{6,7},{7,6},{8,9},{9,8},{10,11... | collective-permute-start | bytes 3145736 | tf_op jit(solution)/shard_map/ppermute | solution.py:382
  86.2 2.3 %collective-permute-done.6.rest = f32[512,512]{1,0:T(8,128)S(1)} collective-permute-done((f32[512,512]{1,0:T(8,128)S(1)}, f32[512,512]{1,0:T(8,128)S(1)}, u32[]{:S(2)}, u32[]{:S(2)}) %collective-permute-start.6) | collective-permute-done | bytes 1048608 | tf_op jit(solution)/shard_map/ppermute | solution.py:382
  88.5 24.5 %next_level.1 = (f32[512,512]{1,0:T(8,128)S(1)}, f32[512,512]{1,0:T(8,128)S(1)}, bf16[2,2,512,512]{3,2,1,0:T(8,128)(2,1)}) custom-call(s32[1]{0:T(128)} %bitcast.core, f32[512,512]{1,0:T(8,128)S(1)} %bitcast.6, f32[512,512]{1,0:T(8,128)S(1)} %collective-permute-done.6.rest, f32[1024,512]{1,0:T(8,128)} %sketch_hbm.3, ...), custom_call_target="tpu_custom_call" | custom-call | tf_op jit(solution)/shard_map/next_level/pallas_call | solution.py:352
  113.1 0.5 collective-permute-start.7
  113.5 2.3 %collective-permute-done.7 = f32[512,512]{1,0:T(8,128)S(1)} collective-permute-done((f32[512,512]{1,0:T(8,128)S(1)}, f32[512,512]{1,0:T(8,128)S(1)}, u32[]{:S(2)}, u32[]{:S(2)}) %collective-permute-start.7) | collective-permute-done | bytes 1048608 | tf_op jit(solution)/shard_map/ppermute | solution.py:382
  115.8 0.2 add.28
  116.0 19.0 %all_to_all.22 = f32[16,32,512]{2,1,0:T(8,128)S(1)} all-to-all(f32[16,32,512]{2,1,0:T(8,128)S(1)} %bitcast.10), channel_id=1, replica_groups=mesh['z'=8,'y'=4,'x'=4,'c'=2] {'y','x'}, dimensions={0} | all-to-all | bytes 2097152 | tf_op jit(solution)/shard_map/all_to_all | solution.py:390
  135.0 0.1 reduce_sum.19
  135.1 0.1 collective-permute-start.8
  135.2 3.1 %collective-permute-done.8 = f32[32,512]{1,0:T(8,128)S(1)} collective-permute-done((f32[32,512]{1,0:T(8,128)S(1)}, f32[32,512]{1,0:T(8,128)S(1)}, u32[]{:S(2)}, u32[]{:S(2)}) %collective-permute-start.8) | collective-permute-done | bytes 65568 | tf_op jit(solution)/shard_map/ppermute | solution.py:397
  138.3 2.0 %collective-permute-start.9 = (f32[32,512]{1,0:T(8,128)S(1)}, f32[32,512]{1,0:T(8,128)S(1)}, u32[]{:S(2)}, u32[]{:S(2)}) collective-permute-start(f32[32,512]{1,0:T(8,128)S(1)} %add.29), channel_id=1, source_target_pairs={{0,64},{32,96},{64,0},{96,32},{128,192},{160,224},{192,128},{224,1... | collective-permute-start | bytes 196616 | tf_op jit(solution)/shard_map/ppermute | solution.py:397
  140.3 2.3 %collective-permute-done.9 = f32[32,512]{1,0:T(8,128)S(1)} collective-permute-done((f32[32,512]{1,0:T(8,128)S(1)}, f32[32,512]{1,0:T(8,128)S(1)}, u32[]{:S(2)}, u32[]{:S(2)}) %collective-permute-start.9) | collective-permute-done | bytes 65568 | tf_op jit(solution)/shard_map/ppermute | solution.py:397
  142.7 3.9 %collective-permute-start.10 = (f32[32,512]{1,0:T(8,128)S(1)}, f32[32,512]{1,0:T(8,128)S(1)}, u32[]{:S(2)}, u32[]{:S(2)}) collective-permute-start(f32[32,512]{1,0:T(8,128)S(1)} %add.30), channel_id=1, source_target_pairs={{0,224},{32,192},{64,160},{96,128},{128,96},{160,64},{192,32},{224... | collective-permute-start | bytes 196616 | tf_op jit(solution)/shard_map/ppermute | solution.py:397
  146.6 2.3 %collective-permute-done.10 = f32[32,512]{1,0:T(8,128)S(1)} collective-permute-done((f32[32,512]{1,0:T(8,128)S(1)}, f32[32,512]{1,0:T(8,128)S(1)}, u32[]{:S(2)}, u32[]{:S(2)}) %collective-permute-start.10) | collective-permute-done | bytes 65568 | tf_op jit(solution)/shard_map/ppermute | solution.py:397
  148.9 0.1 broadcast_in_dim.5
  149.0 15.8 %all_to_all.23 = f32[16,32,512]{2,1,0:T(8,128)S(1)} all-to-all(f32[16,32,512]{2,1,0:T(8,128)S(1)} %broadcast_in_dim.5), channel_id=1, replica_groups=mesh['z'=8,'y'=4,'x'=4,'c'=2] {'y','x'}, dimensions={0} | all-to-all | bytes 2097152 | tf_op jit(solution)/shard_map/all_to_all | solution.py:399
  164.8 5.6 %collective-permute-start.11 = (f32[512,512]{1,0:T(8,128)S(1)}, f32[512,512]{1,0:T(8,128)S(1)}, u32[]{:S(2)}, u32[]{:S(2)}) collective-permute-start(f32[512,512]{1,0:T(8,128)S(1)} %bitcast.7), channel_id=1, source_target_pairs={{0,1},{1,0},{2,3},{3,2},{4,5},{5,4},{6,7},{7,6},{8,9},{9,8},{10,11... | collective-permute-start | bytes 3145736 | tf_op jit(solution)/shard_map/ppermute | solution.py:382
  170.4 2.3 %collective-permute-done.11.rest = f32[512,512]{1,0:T(8,128)S(1)} collective-permute-done((f32[512,512]{1,0:T(8,128)S(1)}, f32[512,512]{1,0:T(8,128)S(1)}, u32[]{:S(2)}, u32[]{:S(2)}) %collective-permute-start.11) | collective-permute-done | bytes 1048608 | tf_op jit(solution)/shard_map/ppermute | solution.py:382
  172.7 19.5 %last_level.1 = f32[512,512]{1,0:T(8,128)} custom-call(s32[1]{0:T(128)} %bitcast.core, f32[512,512]{1,0:T(8,128)S(1)} %bitcast.8, f32[512,512]{1,0:T(8,128)S(1)} %collective-permute-done.11.rest, bf16[2,2,512,512]{3,2,1,0:T(8,128)(2,1)} %get-tuple-element.20.parts_hbm), custom_call_target="tpu_custom_call" | custom-call | tf_op jit(solution)/shard_map/last_level/pallas_call | solution.py:370
  (6 shorter events, 0.1 us)
Async XLA Ops:
  1.3 3.8 %collective-permute-start = (f32[832,128]{1,0:T(8,128)S(1)}, f32[832,128]{1,0:T(8,128)S(1)}, u32[]{:S(2)}, u32[]{:S(2)}) collective-permute-start(f32[832,128]{1,0:T(8,128)S(1)} %get-tuple-element.13), channel_id=1, source_target_pairs={{0,1},{1,0},{2,3},{3,2},{4,5},{5,4},{6,7},{7,6},{8,9},{9,8},{10,11... | collective-permute-start | bytes 1277960 | tf_op jit(solution)/shard_map/ppermute | solution.py:382
  2.1 9.7 %collective-permute-start.1 = (f32[832,128]{1,0:T(8,128)S(1)}, f32[832,128]{1,0:T(8,128)S(1)}, u32[]{:S(2)}, u32[]{:S(2)}) collective-permute-start(f32[832,128]{1,0:T(8,128)S(1)} %get-tuple-element.14), channel_id=1, source_target_pairs={{1,2},{3,4},{5,6},{7,8},{9,10},{11,12},{13,14},{15,16},{17,18},{19... | collective-permute-start | bytes 1277960 | tf_op jit(solution)/shard_map/ppermute | solution.py:406
  11.8 0.7 copy-start
  19.8 6.3 %collective-permute-start.2 = (f32[512,512]{1,0:T(8,128)S(1)}, f32[512,512]{1,0:T(8,128)S(1)}, u32[]{:S(2)}, u32[]{:S(2)}) collective-permute-start(f32[512,512]{1,0:T(8,128)S(1)} %get-tuple-element.16), channel_id=1, source_target_pairs={{0,1},{1,0},{2,3},{3,2},{4,5},{5,4},{6,7},{7,6},{8,9},{9,8},{10,11... | collective-permute-start | bytes 3145736 | tf_op jit(solution)/shard_map/ppermute | solution.py:382
  49.5 3.2 %collective-permute-start.3 = (f32[32,512]{1,0:T(8,128)S(1)}, f32[32,512]{1,0:T(8,128)S(1)}, u32[]{:S(2)}, u32[]{:S(2)}) collective-permute-start(f32[32,512]{1,0:T(8,128)S(1)} %reduce_sum.18), channel_id=1, source_target_pairs={{0,32},{32,0},{64,96},{96,64},{128,160},{160,128},{192,224},{224,1... | collective-permute-start | bytes 196616 | tf_op jit(solution)/shard_map/ppermute | solution.py:397
  52.7 5.9 %collective-permute-start.4 = (f32[32,512]{1,0:T(8,128)S(1)}, f32[32,512]{1,0:T(8,128)S(1)}, u32[]{:S(2)}, u32[]{:S(2)}) collective-permute-start(f32[32,512]{1,0:T(8,128)S(1)} %add.25), channel_id=1, source_target_pairs={{0,64},{32,96},{64,0},{96,32},{128,192},{160,224},{192,128},{224,1... | collective-permute-start | bytes 196616 | tf_op jit(solution)/shard_map/ppermute | solution.py:397
  58.7 6.2 %collective-permute-start.5 = (f32[32,512]{1,0:T(8,128)S(1)}, f32[32,512]{1,0:T(8,128)S(1)}, u32[]{:S(2)}, u32[]{:S(2)}) collective-permute-start(f32[32,512]{1,0:T(8,128)S(1)} %add.26), channel_id=1, source_target_pairs={{0,224},{32,192},{64,160},{96,128},{128,96},{160,64},{192,32},{224... | collective-permute-start | bytes 196616 | tf_op jit(solution)/shard_map/ppermute | solution.py:397
  81.0 7.5 %collective-permute-start.6 = (f32[512,512]{1,0:T(8,128)S(1)}, f32[512,512]{1,0:T(8,128)S(1)}, u32[]{:S(2)}, u32[]{:S(2)}) collective-permute-start(f32[512,512]{1,0:T(8,128)S(1)} %bitcast.5), channel_id=1, source_target_pairs={{0,1},{1,0},{2,3},{3,2},{4,5},{5,4},{6,7},{7,6},{8,9},{9,8},{10,11... | collective-permute-start | bytes 3145736 | tf_op jit(solution)/shard_map/ppermute | solution.py:382
  113.1 2.8 %collective-permute-start.7 = (f32[512,512]{1,0:T(8,128)S(1)}, f32[512,512]{1,0:T(8,128)S(1)}, u32[]{:S(2)}, u32[]{:S(2)}) collective-permute-start(f32[512,512]{1,0:T(8,128)S(1)} %get-tuple-element.19), channel_id=1, source_target_pairs={{0,1},{1,0},{2,3},{3,2},{4,5},{5,4},{6,7},{7,6},{8,9},{9,8},{10,11... | collective-permute-start | bytes 3145736 | tf_op jit(solution)/shard_map/ppermute | solution.py:382
  135.1 3.2 %collective-permute-start.8 = (f32[32,512]{1,0:T(8,128)S(1)}, f32[32,512]{1,0:T(8,128)S(1)}, u32[]{:S(2)}, u32[]{:S(2)}) collective-permute-start(f32[32,512]{1,0:T(8,128)S(1)} %reduce_sum.19), channel_id=1, source_target_pairs={{0,32},{32,0},{64,96},{96,64},{128,160},{160,128},{192,224},{224,1... | collective-permute-start | bytes 196616 | tf_op jit(solution)/shard_map/ppermute | solution.py:397
  138.3 4.3 %collective-permute-start.9 = (f32[32,512]{1,0:T(8,128)S(1)}, f32[32,512]{1,0:T(8,128)S(1)}, u32[]{:S(2)}, u32[]{:S(2)}) collective-permute-start(f32[32,512]{1,0:T(8,128)S(1)} %add.29), channel_id=1, source_target_pairs={{0,64},{32,96},{64,0},{96,32},{128,192},{160,224},{192,128},{224,1... | collective-permute-start | bytes 196616 | tf_op jit(solution)/shard_map/ppermute | solution.py:397
  142.7 6.2 %collective-permute-start.10 = (f32[32,512]{1,0:T(8,128)S(1)}, f32[32,512]{1,0:T(8,128)S(1)}, u32[]{:S(2)}, u32[]{:S(2)}) collective-permute-start(f32[32,512]{1,0:T(8,128)S(1)} %add.30), channel_id=1, source_target_pairs={{0,224},{32,192},{64,160},{96,128},{128,96},{160,64},{192,32},{224... | collective-permute-start | bytes 196616 | tf_op jit(solution)/shard_map/ppermute | solution.py:397
  164.8 7.9 %collective-permute-start.11 = (f32[512,512]{1,0:T(8,128)S(1)}, f32[512,512]{1,0:T(8,128)S(1)}, u32[]{:S(2)}, u32[]{:S(2)}) collective-permute-start(f32[512,512]{1,0:T(8,128)S(1)} %bitcast.7), channel_id=1, source_target_pairs={{0,1},{1,0},{2,3},{3,2},{4,5},{5,4},{6,7},{7,6},{8,9},{9,8},{10,11... | collective-permute-start | bytes 3145736 | tf_op jit(solution)/shard_map/ppermute | solution.py:382

commit v3 on v2

--- a/solution.py
+++ b/solution.py
@@ -138,17 +138,18 @@
     lax.fori_loop(0, count, step, 0)
 
 
-def normal_matrix(own, rest, work_ref):
-    size = work_ref.shape[0]
-    parts = [split3(own), split3(rest)]
+def add_normal(side, into, onto=None):
+    size = into.shape[0]
+    parts = split3(side)
     for at in range(0, size, BLOCK):
         total = jnp.zeros((BLOCK, size - at), F32)
         for i, j in ((1, 1), (2, 0), (0, 2), (1, 0), (0, 1), (0, 0)):
-            for side in parts:
-                total += mul(side[i][:, at : at + BLOCK], side[j][:, at:], (0, 0))
+            total += mul(parts[i][:, at : at + BLOCK], parts[j][:, at:], (0, 0))
+        if onto is not None:
+            total += onto[at : at + BLOCK, at:]
         if at:
-            work_ref[at : at + BLOCK, :at] = jnp.zeros((BLOCK, at), F32)
-        work_ref[at : at + BLOCK, at:] = total
+            into[at : at + BLOCK, :at] = jnp.zeros((BLOCK, at), F32)
+        into[at : at + BLOCK, at:] = total
 
 
 def copies(pairs, sems):
@@ -175,19 +176,16 @@
         move.wait()
 
 
-def powers_body(
-    core, off, near, far, mid_hbm, v_hbm, sketch_hbm, mine, other, parts_hbm, dense, long_ref, mid, v_mid, sketch, parts, sems
-):
+def spread_bands(v, hot, dense, i):
+    block = mul(jnp.concatenate(split2(v), 0), hot, (0, 0))
+    dense[0, i], dense[1, i] = split2(pltpu.roll(block, 0, 1, stride=1, stride_axis=0))
+
+
+def ready_body(off, v_hbm, mid_hbm, sketch_hbm, hot_ref, dense, parts, projected, mid, v_mid, sketch, sems):
     n = BLOCK
-    size = mid.shape[0]
-    width = mid.shape[1]
-    reach = 3 * HALF
-    blocks = size // n + 2
-    c = core[0]
-    fetch = copies(((v_hbm, v_mid), (mid_hbm, mid), (sketch_hbm, sketch)), sems)
+    fetch = copies(((v_hbm, v_mid), (mid_hbm, mid), (sketch_hbm.at[pl.ds(0, mid.shape[0])], sketch)), sems)
     for move in fetch:
         move.start()
-    sides = ((near, 1 - c), (far, c))
     sub = lax.broadcasted_iota(jnp.int32, (8, 2 * n), 0)
     lanes = lax.broadcasted_iota(jnp.int32, (8, 2 * n), 1)
     hot = []
@@ -198,45 +196,86 @@
         hot.append((at + HALF == lanes).astype(F32))
     hot = jnp.concatenate(hot, 0).astype(BF16)
     hot = jnp.concatenate([hot, hot], 0)
-
-    def spread(v, i):
-        block = mul(jnp.concatenate(split2(v), 0), hot, (0, 0))
-        block = pltpu.roll(block, 0, 1, stride=1, stride_axis=0)
-        dense[0, i], dense[1, i] = split2(block)
-
-    for side, below in sides:
+    hot_ref[...] = hot
+    fetch[0].wait()
+    for i in range(dense.shape[1]):
+        spread_bands(v_mid[:, n * i : n * (i + 1)], hot, dense, i)
+    fetch[1].wait()
+    parts[0], parts[1] = split2(mid[...])
+    fetch[2].wait()
+    projected[...] = near_dot((parts[0], parts[1]), split2(sketch[...]))
+
+
+def apply_bands(dense, source, i, n):
+    window = [source[half, n * i : n * i + 2 * n] for half in range(2)]
+    return split2(near_dot((dense[0], dense[1]), window))
+
+
+def first_body(
+    core, near, far, hot, dense, mid, half_projected, sketch_hbm, mine, other, parts_hbm, power, dense_rim, long_ref, sketch, parts, sems
+):
+    n = BLOCK
+    size, width = mid.shape[1:]
+    reach = 3 * HALF
+    inner = size // n
+    c = core[0]
+    fetch, keep, store = copies(
+        ((sketch_hbm.at[pl.ds(size, size)], sketch), (mid, parts_hbm.at[:, 0]), (parts, parts_hbm.at[:, 1])), sems
+    )
+    fetch.start()
+    keep.start()
+    long_ref[:, reach : reach + size] = mid[...]
+    edge = jnp.zeros((2, HALF, width), BF16)
+    power[:, :HALF] = edge
+    power[:, size + 2 * reach - HALF :] = edge
+    for side, below in ((near, 1 - c), (far, c)):
         at = pl.multiple_of(below * (reach + size), HALF)
         for i in range(width // n):
             for half, b in enumerate(split2(side[reach * i : reach * (i + 1)])):
-                long_ref[half, 0, pl.ds(at, reach), n * i : n * (i + 1)] = b
-        spread(side[reach * (width // n) :], below * (blocks - 1))
-    fetch[0].wait()
-    for i in range(1, blocks - 1):
-        spread(v_mid[:, n * (i - 1) : n * i], i)
-    fetch[1].wait()
-    for half, b in enumerate(split2(mid[...])):
-        long_ref[half, 0, reach : reach + size] = b
-        parts[half, 0] = b
-        edge = jnp.zeros((HALF, width), BF16)
-        for level in (1, 2):
-            long_ref[half, level, :HALF] = edge
-            long_ref[half, level, size + 2 * reach - HALF :] = edge
-    store = copies([(parts.at[:, level], parts_hbm.at[:, level]) for level in range(4)], sems.at[pl.ds(3, 4)])
-    store[0].start()
-    for level in range(3):
-        for i in range(blocks) if level < 2 else range(1, blocks - 1):
-            window = [long_ref[half, level, n * i : n * i + 2 * n] for half in range(2)]
-            result = split2(near_dot((dense[0, i], dense[1, i]), window))
-            for half in range(2):
-                if level < 2:
-                    long_ref[half, level + 1, n * i + HALF : n * i + HALF + n] = result[half]
-                if 0 < i < blocks - 1:
-                    parts[half, level + 1, n * (i - 1) : n * i] = result[half]
-        store[level + 1].start()
-    fetch[2].wait()
-    gram_halves(core, parts, sketch, mine, other)
-    for move in store:
-        move.wait()
+                long_ref[half, pl.ds(at, reach), n * i : n * (i + 1)] = b
+        spread_bands(side[reach * (width // n) :], hot[...], dense_rim, below)
+    for i in range(inner + 2):
+        if 0 < i <= inner:
+            block = (dense[0, i - 1], dense[1, i - 1])
+        else:
+            block = (dense_rim[0, i // (inner + 1)], dense_rim[1, i // (inner + 1)])
+        for half, b in enumerate(apply_bands(block, long_ref, i, n)):
+            power[half, n * i + HALF : n * i + HALF + n] = b
+            if 0 < i <= inner:
+                parts[half, n * (i - 1) : n * i] = b
+    store.start()
+    fetch.wait()
+    projected = split2(half_projected[...] + near_dot((parts[0], parts[1]), split2(sketch[...])))
+    keep.wait()
+
+    def gram(first):
+        picked = [jnp.where(first, mid[half], parts[half]) for half in range(2)]
+        return near_dot(picked, projected, (0, 0))
+
+    mine[...] = gram(c == 0)
+    other[...] = gram(c == 1)
+    store.wait()
+
+
+def higher_body(power, dense, dense_rim, parts_hbm, long_ref, parts, sems):
+    n = BLOCK
+    size = parts.shape[2]
+    inner = size // n
+    for level in range(2):
+        source = long_ref if level else power
+        for i in range(level, inner + 2 - level):
+            if 0 < i <= inner:
+                block = (dense[0, i - 1], dense[1, i - 1])
+            else:
+                block = (dense_rim[0, i // (inner + 1)], dense_rim[1, i // (inner + 1)])
+            for half, b in enumerate(apply_bands(block, source, i, n)):
+                if level == 0:
+                    long_ref[half, n * i + HALF : n * i + HALF + n] = b
+                if 0 < i <= inner:
+                    parts[half, level, n * (i - 1) : n * i] = b
+    store = copies(((parts, parts_hbm),), sems)[0]
+    store.start()
+    store.wait()
 
 
 def gram_halves(core, parts, sketch, mine, other):
@@ -249,38 +288,43 @@
     other[...] = near_dot(get(1 - c), projected, (0, 0))
 
 
-def basis_products(core, own, rest, parts, work, row, inv, halves, reached, arrived):
-    c = core[0]
-    normal_matrix(own[...], rest[...], work)
-    halves[0, 0], halves[1, 0] = split2(own[...])
-    halves[0, 1], halves[1, 1] = split2(rest[...])
+def own_body(core, own, *rest):
+    count = len(rest) - 4
+    sources, (normal, reached, parts, sems) = rest[:count], rest[count:]
+    fetch = copies([(src.at[:, core[0]], parts.at[:, s]) for s, src in enumerate(sources)], sems)
+    for move in fetch:
+        move.start()
+    add_normal(own[...], normal)
+    side = split2(own[...])
+    for s in range(count):
+        fetch[s].wait()
+        reached[s] = near_dot((parts[0, s], parts[1, s]), side)
+
+
+def basis_products(core, rest, normal, reached_own, sources, work, row, inv, halves, reached, parts, sems):
+    fetch = copies([(src.at[:, 1 - core[0]], parts.at[:, s]) for s, src in enumerate(sources)], sems)
+    for move in fetch:
+        move.start()
+    add_normal(rest[...], work, normal)
+    halves[0], halves[1] = split2(rest[...])
+    for move in fetch:
+        move.wait()
 
     def beside(b, at):
-        arrived(b)
-        get = lambda s: (parts[0, s, pl.ds(at, BLOCK)], parts[1, s, pl.ds(at, BLOCK)])
-        for s in range(reached.shape[1]):
-            total = near_dot(get(2 * s + c), (halves[0, 0], halves[1, 0]))
-            total += near_dot(get(2 * s + 1 - c), (halves[0, 1], halves[1, 1]))
-            reached[0, s, pl.ds(at, BLOCK)], reached[1, s, pl.ds(at, BLOCK)] = split2(total)
+        rows = pl.ds(at, BLOCK)
+        for s in range(len(sources)):
+            total = reached_own[s, rows] + near_dot((parts[0, s, rows], parts[1, s, rows]), (halves[0], halves[1]))
+            reached[0, s, rows], reached[1, s, rows] = split2(total)
 
     invert_factor(work, row, inv, beside)
 
 
-def share(src, dst, sems, b):
-    rows = pl.ds(pl.multiple_of(b * BLOCK, BLOCK), BLOCK)
-    return pltpu.make_async_copy(src.at[:, :, rows], dst.at[:, :, rows], sems.at[b])
-
-
 def next_body(
-    core, own, rest, sketch_hbm, parts_hbm, mine, other, new_hbm, work, row, inv, halves, reached, parts, sketch, new_parts, sems
+    core, rest, normal, reached_own, sketch_hbm, low_hbm, high_hbm, mine, other, new_hbm, work, row, inv, halves, reached, parts, sems, sketch, new_parts
 ):
-    blocks = parts.shape[2] // BLOCK
-    for b in range(blocks):
-        share(parts_hbm, parts, sems, b).start()
-    fetch, store = copies(((sketch_hbm, sketch), (new_parts, new_hbm)), sems.at[pl.ds(blocks, 2)])
+    fetch, store = copies(((sketch_hbm, sketch), (new_parts, new_hbm)), sems.at[pl.ds(2, 2)])
     fetch.start()
-    arrived = lambda b: share(parts_hbm, parts, sems, b).wait()
-    basis_products(core, own, rest, parts, work, row, inv, halves, reached, arrived)
+    basis_products(core, rest, normal, reached_own, (low_hbm, high_hbm), work, row, inv, halves, reached, parts, sems)
     for s in range(2):
         result = near_dot((reached[0, s], reached[1, s]), (inv[0], inv[1]), (1, 1))
         new_parts[0, s], new_parts[1, s] = split2(result)
@@ -290,11 +334,8 @@
     store.wait()
 
 
-def last_body(core, own, rest, parts_hbm, out, work, row, inv, halves, reached, parts, sems):
-    for b in range(parts.shape[2] // BLOCK):
-        share(parts_hbm, parts, sems, b).start()
-    arrived = lambda b: share(parts_hbm, parts, sems, b).wait()
-    basis_products(core, own, rest, parts, work, row, inv, halves, reached, arrived)
+def last_body(core, rest, normal, reached_own, parts_hbm, out, work, row, inv, halves, reached, parts, sems):
+    basis_products(core, rest, normal, reached_own, (parts_hbm,), work, row, inv, halves, reached, parts, sems)
     out[...] = near_dot((reached[0, 0], reached[1, 0]), (inv[0], inv[1]), (1, 1))
 
 
@@ -307,9 +348,10 @@
         pltpu.VMEM((width, width), F32),
         pltpu.VMEM((BLOCK, width), F32),
         pltpu.VMEM((2, width, width), BF16),
-        pltpu.VMEM((2, 2, width, width), BF16),
+        pltpu.VMEM((2, width, width), BF16),
         pltpu.VMEM((2, count, size, width), BF16),
-        pltpu.VMEM((2, 2 * count, size, width), BF16),
+        pltpu.VMEM((2, count, size, width), BF16),
+        pltpu.SemaphoreType.DMA((4,)),
     ]
 
 
@@ -326,56 +368,79 @@
     )(core, mid, v_mid)
 
 
-def powers(core, off, near, far, mid, v_mid, sketch):
+def kernel(body, name, args, specs, out, out_specs, scratch):
+    return pl.pallas_call(
+        body,
+        out_shape=out,
+        in_specs=specs,
+        out_specs=out_specs,
+        scratch_shapes=scratch,
+        compiler_params=PARAMS,
+        name=name,
+    )(*args)
+
+
+def ready(off, mid, v_mid, sketch):
     size, width = mid.shape
-    return pl.pallas_call(
-        powers_body,
-        out_shape=(shaped(width, width), shaped(width, width), pltpu.HBM((2, 4, size, width), BF16)),
-        in_specs=[SMEM] * 2 + [VMEM] * 2 + [HBM] * 3,
-        out_specs=(VMEM, VMEM, HBM),
-        scratch_shapes=[
-            pltpu.VMEM((2, size // BLOCK + 2, BLOCK, 2 * BLOCK), BF16),
-            pltpu.VMEM((2, 3, size + 6 * HALF, width), BF16),
-            pltpu.VMEM(mid.shape, F32),
-            pltpu.VMEM(v_mid.shape, F32),
-            pltpu.VMEM(sketch.shape, F32),
-            pltpu.VMEM((2, 4, size, width), BF16),
-            pltpu.SemaphoreType.DMA((7,)),
-        ],
-        compiler_params=PARAMS,
-        name="powers",
-    )(core, off, near, far, mid, v_mid, sketch)
-
-
-def next_level(core, own, rest, sketch, parts):
+    out = (
+        shaped(2 * v_mid.shape[0], 2 * BLOCK, dtype=BF16),
+        shaped(2, size // BLOCK, BLOCK, 2 * BLOCK, dtype=BF16),
+        shaped(2, size, width, dtype=BF16),
+        shaped(size, width),
+    )
+    scratch = [pltpu.VMEM(x.shape, F32) for x in (mid, v_mid, mid)] + [pltpu.SemaphoreType.DMA((3,))]
+    return kernel(ready_body, "ready", (off, v_mid, mid, sketch), [SMEM] + [HBM] * 3, out, (VMEM,) * 4, scratch)
+
+
+def first(core, near, far, hot, dense, mid, projected, sketch):
+    size, width = projected.shape
+    out = (
+        shaped(width, width),
+        shaped(width, width),
+        pltpu.HBM((2, 2, size, width), BF16),
+        shaped(2, size + 6 * HALF, width, dtype=BF16),
+        shaped(2, 2, BLOCK, 2 * BLOCK, dtype=BF16),
+    )
+    scratch = [
+        pltpu.VMEM((2, size + 6 * HALF, width), BF16),
+        pltpu.VMEM((size, width), F32),
+        pltpu.VMEM((2, size, width), BF16),
+        pltpu.SemaphoreType.DMA((3,)),
+    ]
+    args = (core, near, far, hot, dense, mid, projected, sketch)
+    return kernel(first_body, "first", args, [SMEM] + [VMEM] * 6 + [HBM], out, (VMEM, VMEM, HBM, VMEM, VMEM), scratch)
+
+
+def higher(power, dense, dense_rim):
+    width = power.shape[2]
+    size = dense.shape[1] * BLOCK
+    scratch = [pltpu.VMEM(power.shape, BF16), pltpu.VMEM((2, 2, size, width), BF16), pltpu.SemaphoreType.DMA((1,))]
+    return kernel(
+        higher_body, "higher", (power, dense, dense_rim), [VMEM] * 3, pltpu.HBM((2, 2, size, width), BF16), HBM, scratch
+    )
+
+
+def own_share(core, own, *sources):
+    size, width = sources[0].shape[2:]
+    count = len(sources)
+    out = (shaped(width, width), shaped(count, size, width))
+    scratch = [pltpu.VMEM((2, count, size, width), BF16), pltpu.SemaphoreType.DMA((count,))]
+    return kernel(own_body, "own_share", (core, own, *sources), [SMEM, VMEM] + [HBM] * count, out, (VMEM,) * 2, scratch)
+
+
+def next_level(core, rest, normal, reached, sketch, low, high):
+    size, width = low.shape[2:]
+    out = (shaped(width, width), shaped(width, width), pltpu.HBM((2, 2, size, width), BF16))
+    scratch = inverse_scratch(size, width, 2) + [pltpu.VMEM(sketch.shape, F32), pltpu.VMEM((2, 2, size, width), BF16)]
+    args = (core, rest, normal, reached, sketch, low, high)
+    return kernel(next_body, "next_level", args, [SMEM] + [VMEM] * 3 + [HBM] * 3, out, (VMEM, VMEM, HBM), scratch)
+
+
+def last_level(core, rest, normal, reached, parts):
     size, width = parts.shape[2:]
-    return pl.pallas_call(
-        next_body,
-        out_shape=(shaped(width, width), shaped(width, width), pltpu.HBM((2, 2, size, width), BF16)),
-        in_specs=[SMEM] + [VMEM] * 2 + [HBM] * 2,
-        out_specs=(VMEM, VMEM, HBM),
-        scratch_shapes=inverse_scratch(size, width, 2)
-        + [
-            pltpu.VMEM(sketch.shape, F32),
-            pltpu.VMEM((2, 2, size, width), BF16),
-            pltpu.SemaphoreType.DMA((size // BLOCK + 2,)),
-        ],
-        compiler_params=PARAMS,
-        name="next_level",
-    )(core, own, rest, sketch, parts)
-
-
-def last_level(core, own, rest, parts):
-    size, width = parts.shape[2:]
-    return pl.pallas_call(
-        last_body,
-        out_shape=shaped(size, width),
-        in_specs=[SMEM] + [VMEM] * 2 + [HBM],
-        out_specs=VMEM,
-        scratch_shapes=inverse_scratch(size, width, 1) + [pltpu.SemaphoreType.DMA((size // BLOCK,))],
-        compiler_params=PARAMS,
-        name="last_level",
-    )(core, own, rest, parts)
+    args = (core, rest, normal, reached, parts)
+    scratch = inverse_scratch(size, width, 1)
+    return kernel(last_body, "last_level", args, [SMEM] + [VMEM] * 3 + [HBM], shaped(size, width), VMEM, scratch)
 
 
 def swap_cores(x):
@@ -406,18 +471,26 @@
     return lax.ppermute(x, ROWS, pairs + [(j, i) for i, j in pairs])
 
 
+def in_hbm(*arrays):
+    return [pltpu.with_memory_space_constraint(x, pltpu.HBM) for x in arrays]
+
+
 def per_device(factor_b, band_vals, offsets, sketch):
     core = lax.axis_index("c").reshape(1)
-    factor_b, band_vals, sketch = (pltpu.with_memory_space_constraint(x, pltpu.HBM) for x in (factor_b, band_vals, sketch))
+    factor_b, band_vals, sketch = in_hbm(factor_b, band_vals, sketch)
     near, far = pack(core, factor_b, band_vals)
     near, far = swap_cores(near), swap_chips(far)
-    mine, other, parts = powers(core, offsets, near, far, factor_b, band_vals, sketch)
+    hot, dense, mid, projected = ready(offsets, factor_b, band_vals, sketch)
+    mine, other, low, power, dense_rim = first(core, near, far, hot, dense, mid, projected, sketch)
+    mine, high = lax.optimization_barrier((mine, higher(power, dense, dense_rim)))
+    low, high = in_hbm(low, high)
     own, rest = sum_over_rows(mine, other)
-    parts = pltpu.with_memory_space_constraint(parts, pltpu.HBM)
-    mine, other, parts = next_level(core, own, rest, sketch, parts)
+    normal, reached = own_share(core, own, low, high)
+    mine, other, parts = next_level(core, rest, normal, reached, sketch, low, high)
     own, rest = sum_over_rows(mine, other)
-    parts = pltpu.with_memory_space_constraint(parts, pltpu.HBM)
-    return last_level(core, own, rest, parts)
+    (parts,) = in_hbm(parts)
+    normal, reached = own_share(core, own, parts)
+    return last_level(core, rest, normal, reached, parts)
 
 
 def solution(mesh):

time: 193 us -> 186 us (0.964)
  waiting for transfers between devices: 30.7 us -> 20.5 us
  Pallas kernels: 52.7 us -> 56.7 us
    ppermute x5, waiting for transfers between devices: 9.15 us -> 2.66 us  [swap_cores(): return lax.ppermute(x, 'c', [(0, 1), (1, 0)])]
    pallas_call x3 -> x7, Pallas kernels: 51.4 us -> 55.4 us  [kernel(): pl.pallas_call(body, out_shape=out, in_specs=specs, out_specs=out_specs,...]
    ppermute x1, waiting for transfers between devices: 6.69 us -> 2.84 us  [swap_chips(): return lax.ppermute(x, ROWS, pairs + [(j, i) for i, j in pairs])]
  transfers between devices with their start and end apart: 12 -> 12, of which waited for: 11 -> 8; matrix products, arithmetic and copies ran while one was open for 0% -> 0% of each run, Pallas kernels for 0% -> 6%
where the time goes in v3:
time: 186 us
  blocking collectives  73.7 us (40%)
  Pallas kernels  56.7 us (30%)
  starting transfers between devices  32.7 us (18%)
  waiting for transfers between devices  20.5 us (11%)
    pallas_call x7, Pallas kernels, kernel(): pl.pallas_call(body, out_shape=out, in_specs=specs, out_specs=out_specs,...  55.4 us
    all_to_all x2, blocking collectives, sum_over_rows(): part = lax.all_to_all(blocks, ('y', 'x'), 0, 0, tiled=True).sum(0)  41.7 us
    all_to_all x2, blocking collectives, sum_over_rows(): lax.all_to_all(copies, ('y', 'x'), 0, 0, tiled=True).reshape(rows, width)  32 us
    ppermute x5, starting transfers between devices, swap_cores(): return lax.ppermute(x, 'c', [(0, 1), (1, 0)])  15.6 us
    ppermute x6, waiting for transfers between devices, sum_over_rows(): part = part + lax.ppermute(part, 'z', pairs)  15 us
    ppermute x6, starting transfers between devices, sum_over_rows(): part = part + lax.ppermute(part, 'z', pairs)  14.1 us
  transfers between devices with their start and end apart: 12, of which 8 were waited for; matrix products, arithmetic and copies ran while one was open for 0% of the time, Pallas kernels for 6%

profile of v3, /device:TPU:33, one launch (start us, length us, event | category | flops | bytes accessed | tf_op | source)
XLA Modules:
  0.0 185.5 jit_solution(4330681575600076076)
XLA Ops:
  0.0 1.3 pack.1
  1.3 0.8 collective-permute-start
  2.1 3.0 %collective-permute-start.1 = (f32[832,128]{1,0:T(8,128)S(1)}, f32[832,128]{1,0:T(8,128)S(1)}, u32[]{:S(2)}, u32[]{:S(2)}) collective-permute-start(f32[832,128]{1,0:T(8,128)S(1)} %get-tuple-element.26), channel_id=1, source_target_pairs={{1,2},{3,4},{5,6},{7,8},{9,10},{11,12},{13,14},{15,16},{17,18},{19... | collective-permute-start | bytes 1277960 | tf_op jit(solution)/shard_map/ppermute | solution.py:471
  5.1 0.0 copy-start
  5.1 0.6 copy-done
  5.8 3.2 %ready.1 = (bf16[128,256]{1,0:T(8,128)(2,1)S(1)}, bf16[2,4,128,256]{3,2,1,0:T(8,128)(2,1)S(1)}, bf16[2,512,512]{2,1,0:T(8,128)(2,1)S(1)}, f32[512,512]{1,0:T(8,128)S(1)}) custom-call(s32[64]{0:T(128)S(1)} %copy-done, f32[64,512]{1,0:T(8,128)} %v_hbm.1, f32[512,512]{1,0:T(8,128)} %mid_hbm.1, f32[1024,512]{1,0:T(8,128)} %sketch_hbm.5), custom_call_target="tpu_custom_call" | custom-call | tf_op jit(solution)/shard_map/ready/pallas_call | solution.py:372
  9.0 0.0 collective-permute-done.near
  9.0 2.8 %collective-permute-done.1.far = f32[832,128]{1,0:T(8,128)S(1)} collective-permute-done((f32[832,128]{1,0:T(8,128)S(1)}, f32[832,128]{1,0:T(8,128)S(1)}, u32[]{:S(2)}, u32[]{:S(2)}) %collective-permute-start.1) | collective-permute-done | bytes 426016 | tf_op jit(solution)/shard_map/ppermute | solution.py:471
  11.8 4.5 %first.1 = (f32[512,512]{1,0:T(8,128)S(1)}, f32[512,512]{1,0:T(8,128)S(1)}, bf16[2,2,512,512]{3,2,1,0:T(8,128)(2,1)}, bf16[2,896,512]{2,1,0:T(8,128)(2,1)S(1)}, bf16[2,2,128,256]{3,2,1,0:T(8,128)(2,1)S(1)}) custom-call(s32[1]{0:T(128)} %bitcast.core, f32[832,128]{1,0:T(8,128)S(1)} %collective-permute-done.near, f32[832,128]{1,0:T(8,128)S(1)} %collective-permute-done.1.far, ...), custom_call_target="tpu_custom_call" | custom-call | tf_op jit(solution)/shard_map/first/pallas_call | solution.py:372
  16.3 4.0 %collective-permute-start.2 = (f32[512,512]{1,0:T(8,128)S(1)}, f32[512,512]{1,0:T(8,128)S(1)}, u32[]{:S(2)}, u32[]{:S(2)}) collective-permute-start(f32[512,512]{1,0:T(8,128)S(1)} %get-tuple-element.35), channel_id=1, source_target_pairs={{0,1},{1,0},{2,3},{3,2},{4,5},{5,4},{6,7},{7,6},{8,9},{9,8},{10,11... | collective-permute-start | bytes 3145736 | tf_op jit(solution)/shard_map/ppermute | solution.py:447
  20.4 2.6 %higher.1.rest_1_.high_hbm = bf16[2,2,512,512]{3,2,1,0:T(8,128)(2,1)} custom-call(bf16[2,896,512]{2,1,0:T(8,128)(2,1)S(1)} %get-tuple-element.32.power, bf16[2,4,128,256]{3,2,1,0:T(8,128)(2,1)S(1)} %get-tuple-element.28.dense, bf16[2,2,128,256]{3,2,1,0:T(8,128)(2,1)S(1)} %get-tuple-element.33.dense_rim), custom_call_target="tpu_custom_call" | custom-call | tf_op jit(solution)/shard_map/higher/pallas_call | solution.py:372
  22.9 0.0 collective-permute-done.2
  22.9 0.2 add.24
  23.2 22.4 %all_to_all.20 = f32[16,32,512]{2,1,0:T(8,128)S(1)} all-to-all(f32[16,32,512]{2,1,0:T(8,128)S(1)} %bitcast.9), channel_id=1, replica_groups=mesh['z'=8,'y'=4,'x'=4,'c'=2] {'y','x'}, dimensions={0} | all-to-all | bytes 2097152 | tf_op jit(solution)/shard_map/all_to_all | solution.py:455
  45.6 0.1 reduce_sum.18
  45.7 0.1 collective-permute-start.3
  45.8 3.1 %collective-permute-done.3 = f32[32,512]{1,0:T(8,128)S(1)} collective-permute-done((f32[32,512]{1,0:T(8,128)S(1)}, f32[32,512]{1,0:T(8,128)S(1)}, u32[]{:S(2)}, u32[]{:S(2)}) %collective-permute-start.3) | collective-permute-done | bytes 65568 | tf_op jit(solution)/shard_map/ppermute | solution.py:462
  48.9 4.3 %collective-permute-start.4 = (f32[32,512]{1,0:T(8,128)S(1)}, f32[32,512]{1,0:T(8,128)S(1)}, u32[]{:S(2)}, u32[]{:S(2)}) collective-permute-start(f32[32,512]{1,0:T(8,128)S(1)} %add.25), channel_id=1, source_target_pairs={{0,64},{32,96},{64,0},{96,32},{128,192},{160,224},{192,128},{224,1... | collective-permute-start | bytes 196616 | tf_op jit(solution)/shard_map/ppermute | solution.py:462
  53.2 1.7 collective-permute-done.4
  54.8 3.8 %collective-permute-start.5 = (f32[32,512]{1,0:T(8,128)S(1)}, f32[32,512]{1,0:T(8,128)S(1)}, u32[]{:S(2)}, u32[]{:S(2)}) collective-permute-start(f32[32,512]{1,0:T(8,128)S(1)} %add.26), channel_id=1, source_target_pairs={{0,224},{32,192},{64,160},{96,128},{128,96},{160,64},{192,32},{224... | collective-permute-start | bytes 196616 | tf_op jit(solution)/shard_map/ppermute | solution.py:462
  58.6 2.4 %collective-permute-done.5 = f32[32,512]{1,0:T(8,128)S(1)} collective-permute-done((f32[32,512]{1,0:T(8,128)S(1)}, f32[32,512]{1,0:T(8,128)S(1)}, u32[]{:S(2)}, u32[]{:S(2)}) %collective-permute-start.5) | collective-permute-done | bytes 65568 | tf_op jit(solution)/shard_map/ppermute | solution.py:462
  61.1 0.1 broadcast_in_dim.4
  61.2 16.2 %all_to_all.21 = f32[16,32,512]{2,1,0:T(8,128)S(1)} all-to-all(f32[16,32,512]{2,1,0:T(8,128)S(1)} %broadcast_in_dim.4), channel_id=1, replica_groups=mesh['z'=8,'y'=4,'x'=4,'c'=2] {'y','x'}, dimensions={0} | all-to-all | bytes 2097152 | tf_op jit(solution)/shard_map/all_to_all | solution.py:464
  77.4 5.3 %collective-permute-start.6 = (f32[512,512]{1,0:T(8,128)S(1)}, f32[512,512]{1,0:T(8,128)S(1)}, u32[]{:S(2)}, u32[]{:S(2)}) collective-permute-start(f32[512,512]{1,0:T(8,128)S(1)} %bitcast.7), channel_id=1, source_target_pairs={{0,1},{1,0},{2,3},{3,2},{4,5},{5,4},{6,7},{7,6},{8,9},{9,8},{10,11... | collective-permute-start | bytes 3145736 | tf_op jit(solution)/shard_map/ppermute | solution.py:447
  82.7 3.6 %own_share.2 = (f32[512,512]{1,0:T(8,128)S(1)}, f32[2,512,512]{2,1,0:T(8,128)S(1)}) custom-call(s32[1]{0:T(128)} %bitcast.core, f32[512,512]{1,0:T(8,128)S(1)} %bitcast.8, bf16[2,2,512,512]{3,2,1,0:T(8,128)(2,1)} %get-tuple-element.36.rest_0_.low_hbm, bf16[2,2,512,512]{3,2,1,0:T(8,128)(2,1)} %higher.1.rest_1_.high_hbm), custom_call_target="tpu_custom_call" | custom-call | tf_op jit(solution)/shard_map/own_share/pallas_call | solution.py:372
  86.4 0.0 collective-permute-done.6.rest
  86.4 21.6 %next_level.1 = (f32[512,512]{1,0:T(8,128)S(1)}, f32[512,512]{1,0:T(8,128)S(1)}, bf16[2,2,512,512]{3,2,1,0:T(8,128)(2,1)}) custom-call(s32[1]{0:T(128)} %bitcast.core, f32[512,512]{1,0:T(8,128)S(1)} %collective-permute-done.6.rest, f32[512,512]{1,0:T(8,128)S(1)} %get-tuple-element.38.normal, f32[2,512,512]{2,1,0:T(8,128)S(1)} %get-tuple-element.39.reached_own, ...), custom_call_target="tpu_custom_call" | custom-call | tf_op jit(solution)/shard_map/next_level/pallas_call | solution.py:372
  108.0 0.1 collective-permute-start.7
  108.1 2.6 %collective-permute-done.7 = f32[512,512]{1,0:T(8,128)S(1)} collective-permute-done((f32[512,512]{1,0:T(8,128)S(1)}, f32[512,512]{1,0:T(8,128)S(1)}, u32[]{:S(2)}, u32[]{:S(2)}) %collective-permute-start.7) | collective-permute-done | bytes 1048608 | tf_op jit(solution)/shard_map/ppermute | solution.py:447
  110.7 0.2 add.28
  110.9 19.3 %all_to_all.22 = f32[16,32,512]{2,1,0:T(8,128)S(1)} all-to-all(f32[16,32,512]{2,1,0:T(8,128)S(1)} %bitcast.10), channel_id=1, replica_groups=mesh['z'=8,'y'=4,'x'=4,'c'=2] {'y','x'}, dimensions={0} | all-to-all | bytes 2097152 | tf_op jit(solution)/shard_map/all_to_all | solution.py:455
  130.2 0.1 reduce_sum.19
  130.3 0.1 collective-permute-start.8
  130.4 3.1 %collective-permute-done.8 = f32[32,512]{1,0:T(8,128)S(1)} collective-permute-done((f32[32,512]{1,0:T(8,128)S(1)}, f32[32,512]{1,0:T(8,128)S(1)}, u32[]{:S(2)}, u32[]{:S(2)}) %collective-permute-start.8) | collective-permute-done | bytes 65568 | tf_op jit(solution)/shard_map/ppermute | solution.py:462
  133.5 2.0 %collective-permute-start.9 = (f32[32,512]{1,0:T(8,128)S(1)}, f32[32,512]{1,0:T(8,128)S(1)}, u32[]{:S(2)}, u32[]{:S(2)}) collective-permute-start(f32[32,512]{1,0:T(8,128)S(1)} %add.29), channel_id=1, source_target_pairs={{0,64},{32,96},{64,0},{96,32},{128,192},{160,224},{192,128},{224,1... | collective-permute-start | bytes 196616 | tf_op jit(solution)/shard_map/ppermute | solution.py:462
  135.5 2.3 %collective-permute-done.9 = f32[32,512]{1,0:T(8,128)S(1)} collective-permute-done((f32[32,512]{1,0:T(8,128)S(1)}, f32[32,512]{1,0:T(8,128)S(1)}, u32[]{:S(2)}, u32[]{:S(2)}) %collective-permute-start.9) | collective-permute-done | bytes 65568 | tf_op jit(solution)/shard_map/ppermute | solution.py:462
  137.8 3.8 %collective-permute-start.10 = (f32[32,512]{1,0:T(8,128)S(1)}, f32[32,512]{1,0:T(8,128)S(1)}, u32[]{:S(2)}, u32[]{:S(2)}) collective-permute-start(f32[32,512]{1,0:T(8,128)S(1)} %add.30), channel_id=1, source_target_pairs={{0,224},{32,192},{64,160},{96,128},{128,96},{160,64},{192,32},{224... | collective-permute-start | bytes 196616 | tf_op jit(solution)/shard_map/ppermute | solution.py:462
  141.6 2.4 %collective-permute-done.10 = f32[32,512]{1,0:T(8,128)S(1)} collective-permute-done((f32[32,512]{1,0:T(8,128)S(1)}, f32[32,512]{1,0:T(8,128)S(1)}, u32[]{:S(2)}, u32[]{:S(2)}) %collective-permute-start.10) | collective-permute-done | bytes 65568 | tf_op jit(solution)/shard_map/ppermute | solution.py:462
  144.1 0.1 broadcast_in_dim.5
  144.2 15.8 %all_to_all.23 = f32[16,32,512]{2,1,0:T(8,128)S(1)} all-to-all(f32[16,32,512]{2,1,0:T(8,128)S(1)} %broadcast_in_dim.5), channel_id=1, replica_groups=mesh['z'=8,'y'=4,'x'=4,'c'=2] {'y','x'}, dimensions={0} | all-to-all | bytes 2097152 | tf_op jit(solution)/shard_map/all_to_all | solution.py:464
  160.0 5.4 %collective-permute-start.11 = (f32[512,512]{1,0:T(8,128)S(1)}, f32[512,512]{1,0:T(8,128)S(1)}, u32[]{:S(2)}, u32[]{:S(2)}) collective-permute-start(f32[512,512]{1,0:T(8,128)S(1)} %bitcast.5), channel_id=1, source_target_pairs={{0,1},{1,0},{2,3},{3,2},{4,5},{5,4},{6,7},{7,6},{8,9},{9,8},{10,11... | collective-permute-start | bytes 3145736 | tf_op jit(solution)/shard_map/ppermute | solution.py:447
  165.4 2.6 %own_share.3 = (f32[512,512]{1,0:T(8,128)S(1)}, f32[1,512,512]{2,1,0:T(8,128)S(1)}) custom-call(s32[1]{0:T(128)} %bitcast.core, f32[512,512]{1,0:T(8,128)S(1)} %bitcast.6, bf16[2,2,512,512]{3,2,1,0:T(8,128)(2,1)} %get-tuple-element.42.rest_0_.parts_hbm), custom_call_target="tpu_custom_call" | custom-call | tf_op jit(solution)/shard_map/own_share/pallas_call | solution.py:372
  168.1 0.0 collective-permute-done.11.rest
  168.1 17.3 %last_level.1 = f32[512,512]{1,0:T(8,128)} custom-call(s32[1]{0:T(128)} %bitcast.core, f32[512,512]{1,0:T(8,128)S(1)} %collective-permute-done.11.rest, f32[512,512]{1,0:T(8,128)S(1)} %get-tuple-element.43.normal, f32[1,512,512]{2,1,0:T(8,128)S(1)} %get-tuple-element.44.reached_own, bf16[2,2,512,512]{3,2,1,0:T(8,128)(2,1)} %get-tuple-element.42.rest_0_.parts_hbm), custom_call_target="tpu_custom_call" | custom-call | tf_op jit(solution)/shard_map/last_level/pallas_call | solution.py:372
  (6 shorter events, 0.1 us)
Async XLA Ops:
  1.3 7.6 %collective-permute-start = (f32[832,128]{1,0:T(8,128)S(1)}, f32[832,128]{1,0:T(8,128)S(1)}, u32[]{:S(2)}, u32[]{:S(2)}) collective-permute-start(f32[832,128]{1,0:T(8,128)S(1)} %get-tuple-element.25), channel_id=1, source_target_pairs={{0,1},{1,0},{2,3},{3,2},{4,5},{5,4},{6,7},{7,6},{8,9},{9,8},{10,11... | collective-permute-start | bytes 1277960 | tf_op jit(solution)/shard_map/ppermute | solution.py:447
  2.1 9.7 %collective-permute-start.1 = (f32[832,128]{1,0:T(8,128)S(1)}, f32[832,128]{1,0:T(8,128)S(1)}, u32[]{:S(2)}, u32[]{:S(2)}) collective-permute-start(f32[832,128]{1,0:T(8,128)S(1)} %get-tuple-element.26), channel_id=1, source_target_pairs={{1,2},{3,4},{5,6},{7,8},{9,10},{11,12},{13,14},{15,16},{17,18},{19... | collective-permute-start | bytes 1277960 | tf_op jit(solution)/shard_map/ppermute | solution.py:471
  5.1 0.7 copy-start
  16.3 6.6 %collective-permute-start.2 = (f32[512,512]{1,0:T(8,128)S(1)}, f32[512,512]{1,0:T(8,128)S(1)}, u32[]{:S(2)}, u32[]{:S(2)}) collective-permute-start(f32[512,512]{1,0:T(8,128)S(1)} %get-tuple-element.35), channel_id=1, source_target_pairs={{0,1},{1,0},{2,3},{3,2},{4,5},{5,4},{6,7},{7,6},{8,9},{9,8},{10,11... | collective-permute-start | bytes 3145736 | tf_op jit(solution)/shard_map/ppermute | solution.py:447
  45.7 3.2 %collective-permute-start.3 = (f32[32,512]{1,0:T(8,128)S(1)}, f32[32,512]{1,0:T(8,128)S(1)}, u32[]{:S(2)}, u32[]{:S(2)}) collective-permute-start(f32[32,512]{1,0:T(8,128)S(1)} %reduce_sum.18), channel_id=1, source_target_pairs={{0,32},{32,0},{64,96},{96,64},{128,160},{160,128},{192,224},{224,1... | collective-permute-start | bytes 196616 | tf_op jit(solution)/shard_map/ppermute | solution.py:462
  48.9 5.9 %collective-permute-start.4 = (f32[32,512]{1,0:T(8,128)S(1)}, f32[32,512]{1,0:T(8,128)S(1)}, u32[]{:S(2)}, u32[]{:S(2)}) collective-permute-start(f32[32,512]{1,0:T(8,128)S(1)} %add.25), channel_id=1, source_target_pairs={{0,64},{32,96},{64,0},{96,32},{128,192},{160,224},{192,128},{224,1... | collective-permute-start | bytes 196616 | tf_op jit(solution)/shard_map/ppermute | solution.py:462
  54.8 6.2 %collective-permute-start.5 = (f32[32,512]{1,0:T(8,128)S(1)}, f32[32,512]{1,0:T(8,128)S(1)}, u32[]{:S(2)}, u32[]{:S(2)}) collective-permute-start(f32[32,512]{1,0:T(8,128)S(1)} %add.26), channel_id=1, source_target_pairs={{0,224},{32,192},{64,160},{96,128},{128,96},{160,64},{192,32},{224... | collective-permute-start | bytes 196616 | tf_op jit(solution)/shard_map/ppermute | solution.py:462
  77.4 9.0 %collective-permute-start.6 = (f32[512,512]{1,0:T(8,128)S(1)}, f32[512,512]{1,0:T(8,128)S(1)}, u32[]{:S(2)}, u32[]{:S(2)}) collective-permute-start(f32[512,512]{1,0:T(8,128)S(1)} %bitcast.7), channel_id=1, source_target_pairs={{0,1},{1,0},{2,3},{3,2},{4,5},{5,4},{6,7},{7,6},{8,9},{9,8},{10,11... | collective-permute-start | bytes 3145736 | tf_op jit(solution)/shard_map/ppermute | solution.py:447
  108.0 2.7 %collective-permute-start.7 = (f32[512,512]{1,0:T(8,128)S(1)}, f32[512,512]{1,0:T(8,128)S(1)}, u32[]{:S(2)}, u32[]{:S(2)}) collective-permute-start(f32[512,512]{1,0:T(8,128)S(1)} %get-tuple-element.41), channel_id=1, source_target_pairs={{0,1},{1,0},{2,3},{3,2},{4,5},{5,4},{6,7},{7,6},{8,9},{9,8},{10,11... | collective-permute-start | bytes 3145736 | tf_op jit(solution)/shard_map/ppermute | solution.py:447
  130.3 3.2 %collective-permute-start.8 = (f32[32,512]{1,0:T(8,128)S(1)}, f32[32,512]{1,0:T(8,128)S(1)}, u32[]{:S(2)}, u32[]{:S(2)}) collective-permute-start(f32[32,512]{1,0:T(8,128)S(1)} %reduce_sum.19), channel_id=1, source_target_pairs={{0,32},{32,0},{64,96},{96,64},{128,160},{160,128},{192,224},{224,1... | collective-permute-start | bytes 196616 | tf_op jit(solution)/shard_map/ppermute | solution.py:462
  133.5 4.3 %collective-permute-start.9 = (f32[32,512]{1,0:T(8,128)S(1)}, f32[32,512]{1,0:T(8,128)S(1)}, u32[]{:S(2)}, u32[]{:S(2)}) collective-permute-start(f32[32,512]{1,0:T(8,128)S(1)} %add.29), channel_id=1, source_target_pairs={{0,64},{32,96},{64,0},{96,32},{128,192},{160,224},{192,128},{224,1... | collective-permute-start | bytes 196616 | tf_op jit(solution)/shard_map/ppermute | solution.py:462
  137.8 6.2 %collective-permute-start.10 = (f32[32,512]{1,0:T(8,128)S(1)}, f32[32,512]{1,0:T(8,128)S(1)}, u32[]{:S(2)}, u32[]{:S(2)}) collective-permute-start(f32[32,512]{1,0:T(8,128)S(1)} %add.30), channel_id=1, source_target_pairs={{0,224},{32,192},{64,160},{96,128},{128,96},{160,64},{192,32},{224... | collective-permute-start | bytes 196616 | tf_op jit(solution)/shard_map/ppermute | solution.py:462
  160.0 8.1 %collective-permute-start.11 = (f32[512,512]{1,0:T(8,128)S(1)}, f32[512,512]{1,0:T(8,128)S(1)}, u32[]{:S(2)}, u32[]{:S(2)}) collective-permute-start(f32[512,512]{1,0:T(8,128)S(1)} %bitcast.5), channel_id=1, source_target_pairs={{0,1},{1,0},{2,3},{3,2},{4,5},{5,4},{6,7},{7,6},{8,9},{9,8},{10,11... | collective-permute-start | bytes 3145736 | tf_op jit(solution)/shard_map/ppermute | solution.py:447
